TPU v7x, 512 devices: a whole 4x8x8 slice. The times are simulated.
512 devices in a mesh: sx: 16 (over z, x_hi), sy: 32 (over y, x_lo, core).
Axes of the slice: x: 4 (x_hi: 2, x_lo: 2; x = x_hi * 2 + x_lo), y: 8, z: 8, core: 2. Of those that a mesh axis runs over, the one named last changes fastest.
Arguments:
- coeffs: float32 [2, 32, 32, 16, 256], P(None, 'sx', 'sy'), may hold values from -6 to 6
- source_nodes: float32 [3, 2, 32, 32, 256], P(None, None, 'sx', 'sy'), may hold values from 0.2 to 1
- target_nodes: float32 [3, 2, 2, 2, 32, 32, 256], P(None, None, None, None, 'sx', 'sy'), may hold values from 0.2 to 1
- interp_rows: float32 [3, 2, 16, 16], replicated, may hold values from -1 to 1
- interp_cols: float32 [3, 2, 16, 16], replicated, may hold values from -1 to 1
Outputs:
- field: float32 [2, 32, 32, 16, 256], P(None, 'sx', 'sy')
All inputs are finite; a program needn't handle non-finite values.
Results may differ from a plain program's by a relative error of at most 0.0003.
Values sent between devices are 32-bit elements; how exact they have to be, the bound alone decides.
No kernel may reach another device: no remote copies, remote signals or barrier semaphores. Data moves between devices by JAX's collectives and lax.ppermute only.
A program may use at most 64 MiB of HBM per device.

v0:
```python
import functools
import math

import jax
import jax.numpy as jnp
import numpy as np
from jax import lax
from jax.experimental import pallas as pl
from jax.experimental.pallas import tpu as pltpu
from jax.sharding import PartitionSpec as P

LEVELS = 3
CHEB = 16
NODES = CHEB * CHEB
RHS = 16
BOXES = 2
FOREIGN = 3
ITEMS = FOREIGN * BOXES
ROOT2 = math.sqrt(2.0)


def half_turn_coefficients():
    nodes = 0.5 * np.cos((np.arange(64) + 0.5) * np.pi / 128)
    powers = np.stack([nodes, nodes**3, nodes**5], axis=1)
    wanted = 2.0**0.75 * np.sin(0.5 * np.pi * nodes)
    return [float(c) for c in np.linalg.lstsq(powers, wanted, rcond=None)[0]]


C0, C1, C2 = half_turn_coefficients()


def group_members(mesh, bit):
    n_rows, n_cols = mesh.shape["sx"], mesh.shape["sy"]
    step = 1 << bit
    groups = []
    for row in range(n_rows):
        for col in range(n_cols):
            if not row & step and not col & step:
                groups.append(
                    [(row + a) * n_cols + col + c for a in (0, step) for c in (0, step)]
                )
    return groups


def fetch(pairs, sems):
    copies = [pltpu.make_async_copy(a, b, sems.at[i]) for i, (a, b) in enumerate(pairs)]
    for copy in copies:
        copy.start()
    return copies


def own_position(level):
    step = 1 << level
    row = lax.axis_index("sx") // step % 2
    col = lax.axis_index("sy") // step % 2
    return 2 * row + col


def prepare(sources, rows, cols, tables):
    a_ref, b_ref, row_ref, col_ref = tables
    lane = lax.broadcasted_iota(jnp.int32, (CHEB, NODES), 1)
    node = lax.broadcasted_iota(jnp.int32, (CHEB, NODES), 0)
    outer = (lane // CHEB == node).astype(jnp.float32)
    inner = (lane % CHEB == node).astype(jnp.float32)
    spread = functools.partial(
        lax.dot_general,
        dimension_numbers=(((0,), (0,)), ((), ())),
        precision=lax.Precision.HIGHEST,
        preferred_element_type=jnp.float32,
    )
    for bit in range(2):
        row_ref[bit] = spread(rows[bit], outer)
        col_ref[bit] = spread(cols[bit], inner)
    lines = []
    for box in range(BOXES):
        freq = sources[0, box]
        slow = sources[1, box]
        near = 16.0 * freq * freq
        lines += [near, near * slow * slow]
    columns = jnp.concatenate(lines + lines, axis=0).T
    for box in range(BOXES):
        a_ref[box] = jnp.broadcast_to(columns[:, 2 * box : 2 * box + 1], (NODES, 128))
        b_ref[box] = jnp.broadcast_to(columns[:, 2 * box + 1 : 2 * box + 2], (NODES, 128))


def weigh(position, box, targets, tables, high, low):
    a_ref, b_ref, row_ref, col_ref = tables
    row_bit, col_bit = position // 2, position % 2
    tau = targets[0, row_bit, col_bit, box]
    off = targets[1, row_bit, col_bit, box]
    tau2, off2 = tau * tau, off * off
    inner = col_ref[col_bit]
    for step in range(CHEB):
        down = pl.ds(step * CHEB, CHEB)
        along = pl.ds(NODES + step * CHEB, CHEB)
        near = a_ref[box, down, :]
        far = b_ref[box, down, :]
        near = jnp.concatenate([near, near], axis=1)
        far = jnp.concatenate([far, far], axis=1)
        kron = row_ref[row_bit, pl.ds(step, 1), :] * inner
        z = near * tau2 + far * off2
        turns = z * lax.rsqrt(z)
        rest = turns - jnp.round(turns)
        y = rest * rest
        half = rest * (C0 + y * (C1 + y * C2))
        q = half * half
        cosine = ROOT2 - q
        v = 2.0 * ROOT2 - q
        sine = half * (v * lax.rsqrt(v))
        part = kron * sine
        real = kron - part * sine
        imag = part * cosine
        for where, value in ((down, real), (along, imag)):
            top = value.astype(jnp.bfloat16)
            high[where, :] = top
            low[where, :] = (value - top.astype(jnp.float32)).astype(jnp.bfloat16)


def stacked(values):
    def turned(x):
        return jnp.concatenate([-x[RHS:], x[:RHS]], axis=0)

    top = values.astype(jnp.bfloat16)
    rest = (values - top.astype(jnp.float32)).astype(jnp.bfloat16)
    left = jnp.concatenate([top, rest], axis=0)
    right = jnp.concatenate([turned(top), turned(rest)], axis=0)
    return jnp.concatenate([left, right], axis=1)


def stack_boxes(real, imag, left):
    for box in range(BOXES):
        left[box] = stacked(jnp.concatenate([real[box], imag[box]], axis=0))


def product(left, high, low):
    main = jnp.dot(left, high, preferred_element_type=jnp.float32)
    small = jnp.dot(left[: 2 * RHS], low, preferred_element_type=jnp.float32)
    return main[: 2 * RHS] + main[2 * RHS :] + small


def put(out, index, box, total):
    out[index, 0, box] = total[:RHS]
    out[index, 1, box] = total[RHS:]


def first_kernel(
    coeffs_hbm, sources_hbm, targets_hbm, rows_hbm, cols_hbm, out_hbm,
    coeffs, sources, targets, rows, cols, *rest,
):
    *tables, high, low, left, stage, in_sems, out_sems = rest
    nodes = fetch(
        [
            (sources_hbm.at[0], sources),
            (rows_hbm.at[0], rows),
            (cols_hbm.at[0], cols),
            (targets_hbm.at[0], targets),
            (coeffs_hbm, coeffs),
        ],
        in_sems,
    )
    me = own_position(0)
    for copy in nodes[:3]:
        copy.wait()
    prepare(sources, rows, cols, tables)
    for copy in nodes[3:]:
        copy.wait()
    stack_boxes(coeffs[0], coeffs[1], left)

    def make(item):
        slot = item % 2
        weigh(me ^ (item // 2 + 1), item % 2, targets, tables, high.at[slot], low.at[slot])

    def use(item):
        slot = item % 2
        put(stage, item // 2, item % 2, product(left[item % 2], high[slot], low[slot]))

    make(0)

    def both(item, carry):
        use(item - 1)
        make(item)
        return carry

    lax.fori_loop(1, ITEMS, both, 0)
    use(ITEMS - 1)
    sent = fetch([(stage.at[x], out_hbm.at[me ^ (x + 1)]) for x in range(FOREIGN)], out_sems)
    for copy in sent:
        copy.wait()


def between_kernel(
    level, values, sources_hbm, targets_hbm, rows_hbm, cols_hbm, own, high, low,
    sources, targets, rows, cols, *rest,
):
    *tables, own_high, own_low, left, sems = rest
    last = level == LEVELS
    count = 1 if last else 2
    here = pl.ds(level - 1, count)
    nodes = fetch(
        [
            (sources_hbm.at[here], sources),
            (rows_hbm.at[here], rows),
            (cols_hbm.at[here], cols),
            (targets_hbm.at[here], targets),
        ],
        sems,
    )
    stack_boxes(values[0], values[1], left)
    for copy in nodes:
        copy.wait()
    prepare(sources.at[0], rows.at[0], cols.at[0], tables)
    me = own_position(level - 1)

    def mine(box, carry):
        weigh(me, box, targets.at[0], tables, own_high, own_low)
        total = product(left[box], own_high[...], own_low[...])
        own[0, box] = total[:RHS]
        own[1, box] = total[RHS:]
        return carry

    lax.fori_loop(0, BOXES, mine, 0)
    if last:
        return
    prepare(sources.at[1], rows.at[1], cols.at[1], tables)
    there = own_position(level)

    def make(item, carry):
        weigh(
            there ^ (item // 2 + 1), item % 2, targets.at[1], tables, high.at[item], low.at[item]
        )
        return carry

    lax.fori_loop(0, ITEMS, make, 0)


def last_between_kernel(values, sources, targets, rows, cols, own, *rest):
    between_kernel(LEVELS, values, sources, targets, rows, cols, own, None, None, *rest)


def summed(level, pieces, own):
    me = own_position(level)
    return (own[...] + pieces[me ^ 1]) + (pieces[me ^ 2] + pieces[me ^ 3])


def later_kernel(level, pieces, own, high, low, out_hbm, current, left, stage, sems):
    values = summed(level - 1, pieces, own)
    current[...] = values
    stack_boxes(values[0], values[1], left)
    me = own_position(level)
    sent = []
    for x in range(FOREIGN):
        for box in range(BOXES):
            item = 2 * x + box
            put(stage, x, box, product(left[box], high[item], low[item]))
        copy = pltpu.make_async_copy(stage.at[x], out_hbm.at[me ^ (x + 1)], sems.at[x])
        copy.start()
        sent.append(copy)
    for copy in sent:
        copy.wait()


def final_kernel(pieces, own, out):
    out[...] = summed(LEVELS - 1, pieces, own)


def node_buffers(count):
    lead = () if count is None else (count,)
    return (
        pltpu.VMEM(lead + (2, BOXES, 1, NODES), jnp.float32),
        pltpu.VMEM(lead + (2, 2, 2, BOXES, 1, NODES), jnp.float32),
        pltpu.VMEM(lead + (2, CHEB, CHEB), jnp.float32),
        pltpu.VMEM(lead + (2, CHEB, CHEB), jnp.float32),
    )


TABLES = (
    pltpu.VMEM((BOXES, NODES, 128), jnp.float32),
    pltpu.VMEM((BOXES, NODES, 128), jnp.float32),
    pltpu.VMEM((2, CHEB, NODES), jnp.float32),
    pltpu.VMEM((2, CHEB, NODES), jnp.float32),
)
FIELD = (2, BOXES, RHS, NODES)
LEFT = pltpu.VMEM((BOXES, 4 * RHS, 2 * NODES), jnp.bfloat16)
STAGE = pltpu.VMEM((FOREIGN,) + FIELD, jnp.float32)
ANY = pl.BlockSpec(memory_space=pltpu.HBM)
WHOLE = pl.BlockSpec(memory_space=pltpu.VMEM)
PARAMS = pltpu.CompilerParams(vmem_limit_bytes=12 * 1024 * 1024)


SENT = pltpu.HBM((4,) + FIELD, jnp.float32)
KEPT = pltpu.VMEM(FIELD, jnp.float32)
MADE = pltpu.VMEM((ITEMS, 2 * NODES, NODES), jnp.bfloat16)


def far(x):
    return pltpu.with_memory_space_constraint(x, pltpu.HBM)


def cost(flops):
    return pl.CostEstimate(flops=flops, bytes_accessed=100_000, transcendentals=0)


def solution(mesh):
    groups = [group_members(mesh, bit) for bit in range(LEVELS)]

    def exchange(sent, level):
        return lax.all_to_all(
            sent, ("sx", "sy"), 0, 0, axis_index_groups=groups[level], tiled=True
        )

    def local(coeffs, source_nodes, target_nodes, interp_rows, interp_cols):
        current = coeffs.reshape(FIELD)
        nodes = (
            far(source_nodes.reshape(LEVELS, 2, BOXES, 1, NODES)),
            far(target_nodes.reshape(LEVELS, 2, 2, 2, BOXES, 1, NODES)),
            far(interp_rows),
            far(interp_cols),
        )
        sent = pl.pallas_call(
            first_kernel,
            in_specs=[ANY] * 5,
            out_specs=ANY,
            out_shape=SENT,
            scratch_shapes=(pltpu.VMEM(FIELD, jnp.float32),)
            + node_buffers(None)
            + TABLES
            + (pltpu.VMEM((2, 2 * NODES, NODES), jnp.bfloat16),) * 2
            + (LEFT, STAGE, pltpu.SemaphoreType.DMA((5,)), pltpu.SemaphoreType.DMA((FOREIGN,))),
            compiler_params=PARAMS,
            name="first",
        )(far(current), *nodes)
        for level in range(1, LEVELS + 1):
            last = level == LEVELS
            made = pl.pallas_call(
                last_between_kernel if last else functools.partial(between_kernel, level),
                in_specs=[WHOLE] + [ANY] * 4,
                out_specs=[WHOLE] * (1 if last else 3),
                out_shape=[KEPT] + ([] if last else [MADE] * 2),
                scratch_shapes=node_buffers(1 if last else 2)
                + TABLES
                + (pltpu.VMEM((2 * NODES, NODES), jnp.bfloat16),) * 2
                + (LEFT, pltpu.SemaphoreType.DMA((4,))),
                compiler_params=PARAMS,
                cost_estimate=cost(60_000_000),
                name=f"between_{level}",
            )(current, *nodes)
            pieces = exchange(sent, level - 1)
            if last:
                break
            sent, current = pl.pallas_call(
                functools.partial(later_kernel, level),
                in_specs=[WHOLE] * 4,
                out_specs=[ANY, WHOLE],
                out_shape=[SENT, KEPT],
                scratch_shapes=(LEFT, STAGE, pltpu.SemaphoreType.DMA((FOREIGN,))),
                compiler_params=PARAMS,
                name=f"later_{level}",
            )(pieces, *made)
        field = pl.pallas_call(
            final_kernel,
            in_specs=[WHOLE] * 2,
            out_specs=WHOLE,
            out_shape=jax.ShapeDtypeStruct(FIELD, jnp.float32),
            compiler_params=PARAMS,
            name="final",
        )(pieces, *made)
        return field.reshape(2, BOXES, 1, RHS, NODES)

    in_specs = (
        P(None, "sx", "sy", None, None),
        P(None, None, "sx", "sy", None),
        P(None, None, None, None, "sx", "sy", None),
        P(),
        P(),
    )
    out_specs = P(None, "sx", "sy", None, None)
    return jax.shard_map(local, mesh=mesh, in_specs=in_specs, out_specs=out_specs, check_vma=False)
```

profile of v0, /device:TPU:2, one launch (start us, length us, event | category | flops | bytes accessed | tf_op | source)
XLA Modules:
  0.0 43.6 jit_solution(17642771847798129786)
XLA Ops:
  0.0 3.9 %first.1 = f32[4,2,2,16,256]{4,3,2,1,0:T(8,128)} custom-call(f32[2,2,16,256]{3,2,1,0:T(8,128)} %bitcast.4, f32[3,2,2,1,256]{4,3,2,1,0:T(1,128)} %sources.1, f32[3,2,2,2,2,1,256]{6,5,4,3,2,1,0:T(1,128)} %targets.1, f32[3,2,16,16]{3,2,1,0:T(8,128)} %rows.1, f32[3,2,16,16]{3,2,1,0:T(8,128)} %cols.1), custom_call_target="tpu_custom_call" | custom-call | tf_op jit(solution)/shard_map/first/pallas_call | solution.py:319
  3.9 3.4 %all-to-all-start = ((f32[4,2,2,16,256]{4,3,2,1,0:T(8,128)}), f32[4,2,2,16,256]{4,3,2,1,0:T(8,128)S(1)}, u32[]{:S(2)}, u32[]{:S(2)}) async-start(f32[4,2,2,16,256]{4,3,2,1,0:T(8,128)} %first.1), calls=%async_computation | async-start | bytes 524288 | tf_op jit(solution)/shard_map/all_to_all | solution.py:307
  7.3 0.0 copy-start
  7.3 0.8 %copy-done = f32[2,2,1,16,256]{4,3,2,1,0:T(8,128)S(1)} copy-done((f32[2,2,1,16,256]{4,3,2,1,0:T(8,128)S(1)}, f32[2,2,1,16,256]{4,3,2,1,0:T(8,128)}, u32[]{:S(2)}) %copy-start) | copy-done | bytes 65560
  8.2 4.1 %between_1.1 = (f32[2,2,16,256]{3,2,1,0:T(8,128)S(1)}, bf16[6,512,256]{2,1,0:T(8,128)(2,1)S(1)}, bf16[6,512,256]{2,1,0:T(8,128)(2,1)S(1)}) custom-call(f32[2,2,16,256]{3,2,1,0:T(8,128)S(1)} %bitcast.5, f32[3,2,2,1,256]{4,3,2,1,0:T(1,128)} %sources.1, f32[3,2,2,2,2,1,256]{6,5,4,3,2,1,0:T(1,128)} %targets.1, f32[3,2,16,16]{3,2,1,0:T(8,128)} %rows.1, ...), custom_call_target="tpu_custom_call" | custom-call | flops 60000000 | bytes 100000 | tf_op jit(solution)/shard_map/between_1/pallas_call | solution.py:334
  12.2 2.6 %all-to-all-done.pieces = f32[4,2,2,16,256]{4,3,2,1,0:T(8,128)S(1)} async-done(((f32[4,2,2,16,256]{4,3,2,1,0:T(8,128)}), f32[4,2,2,16,256]{4,3,2,1,0:T(8,128)S(1)}, u32[]{:S(2)}, u32[]{:S(2)}) %all-to-all-start) | async-done | bytes 262176 | tf_op jit(solution)/shard_map/all_to_all | solution.py:307
  14.8 1.3 %later_1.1 = (f32[4,2,2,16,256]{4,3,2,1,0:T(8,128)}, f32[2,2,16,256]{3,2,1,0:T(8,128)S(1)}) custom-call(f32[4,2,2,16,256]{4,3,2,1,0:T(8,128)S(1)} %all-to-all-done.pieces, f32[2,2,16,256]{3,2,1,0:T(8,128)S(1)} %get-tuple-element.15.own, bf16[6,512,256]{2,1,0:T(8,128)(2,1)S(1)} %get-tuple-element.16.high, bf16[6,512,256]{2,1,0:T(8,128)(2,1)S(1)} %get-tuple-element.17.low), custom_call_target="tpu_custom_call" | custom-call | tf_op jit(solution)/shard_map/later_1/pallas_call | solution.py:350
  16.1 9.2 %all-to-all-start.1 = ((f32[4,2,2,16,256]{4,3,2,1,0:T(8,128)}), f32[4,2,2,16,256]{4,3,2,1,0:T(8,128)S(1)}, u32[]{:S(2)}, u32[]{:S(2)}) async-start(f32[4,2,2,16,256]{4,3,2,1,0:T(8,128)} %get-tuple-element.18), calls=%async_computation.1 | async-start | bytes 524288 | tf_op jit(solution)/shard_map/all_to_all | solution.py:307
  25.3 4.1 %between_2.1 = (f32[2,2,16,256]{3,2,1,0:T(8,128)S(1)}, bf16[6,512,256]{2,1,0:T(8,128)(2,1)S(1)}, bf16[6,512,256]{2,1,0:T(8,128)(2,1)S(1)}) custom-call(f32[2,2,16,256]{3,2,1,0:T(8,128)S(1)} %get-tuple-element.19.values, f32[3,2,2,1,256]{4,3,2,1,0:T(1,128)} %sources.1, f32[3,2,2,2,2,1,256]{6,5,4,3,2,1,0:T(1,128)} %targets.1, f32[3,2,16,16]{3,2,1,0:T(8,128)} %rows.1, ...), custom_call_target="tpu_custom_call" | custom-call | flops 60000000 | bytes 100000 | tf_op jit(solution)/shard_map/between_2/pallas_call | solution.py:334
  29.4 0.5 %all-to-all-done.1.pieces = f32[4,2,2,16,256]{4,3,2,1,0:T(8,128)S(1)} async-done(((f32[4,2,2,16,256]{4,3,2,1,0:T(8,128)}), f32[4,2,2,16,256]{4,3,2,1,0:T(8,128)S(1)}, u32[]{:S(2)}, u32[]{:S(2)}) %all-to-all-start.1) | async-done | bytes 262176 | tf_op jit(solution)/shard_map/all_to_all | solution.py:307
  30.0 1.3 %later_2.1 = (f32[4,2,2,16,256]{4,3,2,1,0:T(8,128)}, f32[2,2,16,256]{3,2,1,0:T(8,128)S(1)}) custom-call(f32[4,2,2,16,256]{4,3,2,1,0:T(8,128)S(1)} %all-to-all-done.1.pieces, f32[2,2,16,256]{3,2,1,0:T(8,128)S(1)} %get-tuple-element.20.own, bf16[6,512,256]{2,1,0:T(8,128)(2,1)S(1)} %get-tuple-element.21.high, bf16[6,512,256]{2,1,0:T(8,128)(2,1)S(1)} %get-tuple-element.22.low), custom_call_target="tpu_custom_call" | custom-call | tf_op jit(solution)/shard_map/later_2/pallas_call | solution.py:350
  31.3 3.4 %all-to-all-start.2 = ((f32[4,2,2,16,256]{4,3,2,1,0:T(8,128)}), f32[4,2,2,16,256]{4,3,2,1,0:T(8,128)S(1)}, u32[]{:S(2)}, u32[]{:S(2)}) async-start(f32[4,2,2,16,256]{4,3,2,1,0:T(8,128)} %get-tuple-element.23), calls=%async_computation.2 | async-start | bytes 524288 | tf_op jit(solution)/shard_map/all_to_all | solution.py:307
  34.7 2.0 %between_3.1.own = f32[2,2,16,256]{3,2,1,0:T(8,128)S(1)} custom-call(f32[2,2,16,256]{3,2,1,0:T(8,128)S(1)} %get-tuple-element.24.values, f32[3,2,2,1,256]{4,3,2,1,0:T(1,128)} %sources.1, f32[3,2,2,2,2,1,256]{6,5,4,3,2,1,0:T(1,128)} %targets.1, f32[3,2,16,16]{3,2,1,0:T(8,128)} %rows.1, f32[3,2,16,16]{3,2,1,0:T(8,128)} %cols.1), custom_call_target="tpu_custom_call" | custom-call | flops 60000000 | bytes 100000 | tf_op jit(solution)/shard_map/between_3/pallas_call | solution.py:334
  36.7 6.2 %all-to-all-done.2.pieces = f32[4,2,2,16,256]{4,3,2,1,0:T(8,128)S(1)} async-done(((f32[4,2,2,16,256]{4,3,2,1,0:T(8,128)}), f32[4,2,2,16,256]{4,3,2,1,0:T(8,128)S(1)}, u32[]{:S(2)}, u32[]{:S(2)}) %all-to-all-start.2) | async-done | bytes 262176 | tf_op jit(solution)/shard_map/all_to_all | solution.py:307
  42.9 0.6 %final.1 = f32[2,2,16,256]{3,2,1,0:T(8,128)} custom-call(f32[4,2,2,16,256]{4,3,2,1,0:T(8,128)S(1)} %all-to-all-done.2.pieces, f32[2,2,16,256]{3,2,1,0:T(8,128)S(1)} %between_3.1.own), custom_call_target="tpu_custom_call" | custom-call | tf_op jit(solution)/shard_map/final/pallas_call | solution.py:359
Async XLA Ops:
  3.9 10.9 %all-to-all-start = ((f32[4,2,2,16,256]{4,3,2,1,0:T(8,128)}), f32[4,2,2,16,256]{4,3,2,1,0:T(8,128)S(1)}, u32[]{:S(2)}, u32[]{:S(2)}) async-start(f32[4,2,2,16,256]{4,3,2,1,0:T(8,128)} %first.1), calls=%async_computation | async-start | bytes 524288 | tf_op jit(solution)/shard_map/all_to_all | solution.py:307
  7.3 0.8 %copy-start = (f32[2,2,1,16,256]{4,3,2,1,0:T(8,128)S(1)}, f32[2,2,1,16,256]{4,3,2,1,0:T(8,128)}, u32[]{:S(2)}) copy-start(f32[2,2,1,16,256]{4,3,2,1,0:T(8,128)} %param.5) | copy-start | bytes 196612
  16.1 13.9 %all-to-all-start.1 = ((f32[4,2,2,16,256]{4,3,2,1,0:T(8,128)}), f32[4,2,2,16,256]{4,3,2,1,0:T(8,128)S(1)}, u32[]{:S(2)}, u32[]{:S(2)}) async-start(f32[4,2,2,16,256]{4,3,2,1,0:T(8,128)} %get-tuple-element.18), calls=%async_computation.1 | async-start | bytes 524288 | tf_op jit(solution)/shard_map/all_to_all | solution.py:307
  31.3 11.6 %all-to-all-start.2 = ((f32[4,2,2,16,256]{4,3,2,1,0:T(8,128)}), f32[4,2,2,16,256]{4,3,2,1,0:T(8,128)S(1)}, u32[]{:S(2)}, u32[]{:S(2)}) async-start(f32[4,2,2,16,256]{4,3,2,1,0:T(8,128)} %get-tuple-element.23), calls=%async_computation.2 | async-start | bytes 524288 | tf_op jit(solution)/shard_map/all_to_all | solution.py:307
where the time goes:
time: 44.2 us; the launch traced here: 43.6 us
  Pallas kernels  17.2 us (39%)
  starting transfers between devices  16.1 us (36%)
  waiting for transfers between devices  9.33 us (21%)
  local copies, waits for them, and re-layouts  0.83 us (2%)
    all_to_all x3, starting transfers between devices, exchange(): lax.all_to_all(sent, ('sx', 'sy'), 0, 0, axis_index_groups=groups[level],...  16.1 us
    pallas_call x3, Pallas kernels, local(): pl.pallas_call(last_between_kernel if last else functools.partial(between...  10.1 us
    all_to_all x3, waiting for transfers between devices, exchange(): lax.all_to_all(sent, ('sx', 'sy'), 0, 0, axis_index_groups=groups[level],...  9.33 us
    pallas_call x1, Pallas kernels, local(): pl.pallas_call(first_kernel, in_specs=[ANY] * 5, out_specs=ANY, out_shape...  3.89 us
    pallas_call x2, Pallas kernels, local(): pl.pallas_call(functools.partial(later_kernel, level), in_specs=[WHOLE] *...  2.58 us
  transfers between devices with their start and end apart: 3, of which 3 were waited for; matrix products, arithmetic and copies ran while one was open for 0% of the time, Pallas kernels for 23%

commit v1 on v0

--- a/solution.py
+++ b/solution.py
@@ -17,6 +17,9 @@
 FOREIGN = 3
 ITEMS = FOREIGN * BOXES
 ROOT2 = math.sqrt(2.0)
+SOURCE_LINE = 2 * BOXES * RHS
+TARGET_LINE = SOURCE_LINE + 2 * BOXES
+PACKED = 88
 
 
 def half_turn_coefficients():
@@ -42,6 +45,11 @@
     return groups
 
 
+def swapped(block, axis):
+    count = lax.axis_size(axis)
+    return lax.ppermute(block, axis, [(i, i ^ 1) for i in range(count)])
+
+
 def fetch(pairs, sems):
     copies = [pltpu.make_async_copy(a, b, sems.at[i]) for i, (a, b) in enumerate(pairs)]
     for copy in copies:
@@ -56,8 +64,7 @@
     return 2 * row + col
 
 
-def prepare(sources, rows, cols, tables):
-    a_ref, b_ref, row_ref, col_ref = tables
+def spread_matrices(rows, cols, row_ref, col_ref):
     lane = lax.broadcasted_iota(jnp.int32, (CHEB, NODES), 1)
     node = lax.broadcasted_iota(jnp.int32, (CHEB, NODES), 0)
     outer = (lane // CHEB == node).astype(jnp.float32)
@@ -71,10 +78,13 @@
     for bit in range(2):
         row_ref[bit] = spread(rows[bit], outer)
         col_ref[bit] = spread(cols[bit], inner)
+
+
+def spread_sources(source, a_ref, b_ref):
     lines = []
     for box in range(BOXES):
-        freq = sources[0, box]
-        slow = sources[1, box]
+        freq = source(0, box)
+        slow = source(1, box)
         near = 16.0 * freq * freq
         lines += [near, near * slow * slow]
     columns = jnp.concatenate(lines + lines, axis=0).T
@@ -83,11 +93,21 @@
         b_ref[box] = jnp.broadcast_to(columns[:, 2 * box + 1 : 2 * box + 2], (NODES, 128))
 
 
-def weigh(position, box, targets, tables, high, low):
+def prepare(sources, rows, cols, tables):
+    a_ref, b_ref, row_ref, col_ref = tables
+    spread_matrices(rows, cols, row_ref, col_ref)
+    spread_sources(lambda kind, box: sources[kind, box], a_ref, b_ref)
+
+
+def line_of(targets):
+    return lambda kind, row_bit, col_bit, box: targets[kind, row_bit, col_bit, box]
+
+
+def weigh(position, box, target, tables, high, low):
     a_ref, b_ref, row_ref, col_ref = tables
     row_bit, col_bit = position // 2, position % 2
-    tau = targets[0, row_bit, col_bit, box]
-    off = targets[1, row_bit, col_bit, box]
+    tau = target(0, row_bit, col_bit, box)
+    off = target(1, row_bit, col_bit, box)
     tau2, off2 = tau * tau, off * off
     inner = col_ref[col_bit]
     for step in range(CHEB):
@@ -143,49 +163,131 @@
     out[index, 1, box] = total[RHS:]
 
 
-def first_kernel(
-    coeffs_hbm, sources_hbm, targets_hbm, rows_hbm, cols_hbm, out_hbm,
-    coeffs, sources, targets, rows, cols, *rest,
+def packed_source(packed):
+    return lambda kind, box: packed[pl.ds(SOURCE_LINE + 2 * kind + box, 1), :]
+
+
+def packed_target(packed):
+    def line(kind, row_bit, col_bit, box):
+        place = ((kind * 2 + row_bit) * 2 + col_bit) * BOXES + box
+        return packed[pl.ds(TARGET_LINE + place, 1), :]
+
+    return line
+
+
+def packed_values(packed, box):
+    real = packed[box * RHS : (box + 1) * RHS, :]
+    imag = packed[(BOXES + box) * RHS : (BOXES + box + 1) * RHS, :]
+    return jnp.concatenate([real, imag], axis=0)
+
+
+def pack_kernel(
+    coeffs_hbm, sources_hbm, targets_hbm, rows_hbm, cols_hbm, packed, rows, cols,
+    coeffs, sources, targets, sems,
 ):
-    *tables, high, low, left, stage, in_sems, out_sems = rest
+    copies = fetch(
+        [
+            (coeffs_hbm, coeffs),
+            (sources_hbm.at[0], sources),
+            (targets_hbm.at[0], targets),
+            (rows_hbm.at[0], rows),
+            (cols_hbm.at[0], cols),
+        ],
+        sems,
+    )
+    for copy in copies:
+        copy.wait()
+    for part in range(2):
+        for box in range(BOXES):
+            packed[pl.ds((part * BOXES + box) * RHS, RHS), :] = coeffs[part, box]
+    lines = [sources[kind, box] for kind in range(2) for box in range(BOXES)]
+    for kind in range(2):
+        for place in range(4 * BOXES):
+            lines.append(targets[kind, place // 4, place // 2 % 2, place % 2])
+    lines += [lines[-1]] * (PACKED - SOURCE_LINE - len(lines))
+    packed[pl.ds(SOURCE_LINE, PACKED - SOURCE_LINE), :] = jnp.concatenate(lines, axis=0)
+
+
+def pair_of_boxes(packed, position, tables, high, low):
+    target = packed_target(packed)
+    for box in range(BOXES):
+        weigh(position, box, target, tables, high.at[box], low.at[box])
+    return [
+        product(stacked(packed_values(packed, box)), high[box], low[box]) for box in range(BOXES)
+    ]
+
+
+def near_kernel(packed, rows, cols, partial, row_ref, col_ref, a_ref, b_ref, high, low):
+    spread_matrices(rows, cols, row_ref, col_ref)
+    spread_sources(packed_source(packed), a_ref, b_ref)
+    tables = (a_ref, b_ref, row_ref, col_ref)
+    both = pair_of_boxes(packed, own_position(0) ^ 2, tables, high, low)
+    for box in range(BOXES):
+        partial[0, box] = both[box][:RHS]
+        partial[1, box] = both[box][RHS:]
+
+
+def partner_kernel(packed, row_ref, col_ref, partial, sent, a_ref, b_ref, high, low):
+    spread_sources(packed_source(packed), a_ref, b_ref)
+    tables = (a_ref, b_ref, row_ref, col_ref)
+    both = pair_of_boxes(packed, own_position(0) ^ 2, tables, high, low)
+    for box in range(BOXES):
+        sent[0, box] = partial[0, box] + both[box][:RHS]
+        sent[1, box] = partial[1, box] + both[box][RHS:]
+
+
+def foreign_weights(level, targets, tables, high, low):
+    there = own_position(level)
+
+    def make(item, carry):
+        weigh(
+            there ^ (item // 2 + 1), item % 2, line_of(targets), tables, high.at[item], low.at[item]
+        )
+        return carry
+
+    lax.fori_loop(0, ITEMS, make, 0)
+
+
+def second_kernel(
+    packed, got, row0_ref, col0_ref, sources_hbm, targets_hbm, rows_hbm, cols_hbm, own, high, low,
+    sources, targets, rows, cols, *rest,
+):
+    a_ref, b_ref, row_ref, col_ref, own_high, own_low, sems = rest
     nodes = fetch(
         [
-            (sources_hbm.at[0], sources),
-            (rows_hbm.at[0], rows),
-            (cols_hbm.at[0], cols),
-            (targets_hbm.at[0], targets),
-            (coeffs_hbm, coeffs),
+            (sources_hbm.at[1], sources),
+            (rows_hbm.at[1], rows),
+            (cols_hbm.at[1], cols),
+            (targets_hbm.at[1], targets),
         ],
-        in_sems,
+        sems,
     )
     me = own_position(0)
-    for copy in nodes[:3]:
+    tables = (a_ref, b_ref, row0_ref, col0_ref)
+    for index, lines in enumerate((packed, got)):
+        spread_sources(packed_source(lines), a_ref, b_ref)
+
+        def mine(box, carry):
+            weigh(me, box, packed_target(lines), tables, own_high, own_low)
+            start = pl.multiple_of(box * RHS, RHS)
+            real = lines[pl.ds(start, RHS), :]
+            imag = lines[pl.ds(start + BOXES * RHS, RHS), :]
+            left = stacked(jnp.concatenate([real, imag], axis=0))
+            total = product(left, own_high[...], own_low[...])
+            if index:
+                own[0, box] += total[:RHS]
+                own[1, box] += total[RHS:]
+            else:
+                own[0, box] = total[:RHS]
+                own[1, box] = total[RHS:]
+            return carry
+
+        lax.fori_loop(0, BOXES, mine, 0)
+    for copy in nodes:
         copy.wait()
+    tables = (a_ref, b_ref, row_ref, col_ref)
     prepare(sources, rows, cols, tables)
-    for copy in nodes[3:]:
-        copy.wait()
-    stack_boxes(coeffs[0], coeffs[1], left)
-
-    def make(item):
-        slot = item % 2
-        weigh(me ^ (item // 2 + 1), item % 2, targets, tables, high.at[slot], low.at[slot])
-
-    def use(item):
-        slot = item % 2
-        put(stage, item // 2, item % 2, product(left[item % 2], high[slot], low[slot]))
-
-    make(0)
-
-    def both(item, carry):
-        use(item - 1)
-        make(item)
-        return carry
-
-    lax.fori_loop(1, ITEMS, both, 0)
-    use(ITEMS - 1)
-    sent = fetch([(stage.at[x], out_hbm.at[me ^ (x + 1)]) for x in range(FOREIGN)], out_sems)
-    for copy in sent:
-        copy.wait()
+    foreign_weights(1, targets, tables, high, low)
 
 
 def between_kernel(
@@ -212,7 +314,7 @@
     me = own_position(level - 1)
 
     def mine(box, carry):
-        weigh(me, box, targets.at[0], tables, own_high, own_low)
+        weigh(me, box, line_of(targets.at[0]), tables, own_high, own_low)
         total = product(left[box], own_high[...], own_low[...])
         own[0, box] = total[:RHS]
         own[1, box] = total[RHS:]
@@ -222,15 +324,7 @@
     if last:
         return
     prepare(sources.at[1], rows.at[1], cols.at[1], tables)
-    there = own_position(level)
-
-    def make(item, carry):
-        weigh(
-            there ^ (item // 2 + 1), item % 2, targets.at[1], tables, high.at[item], low.at[item]
-        )
-        return carry
-
-    lax.fori_loop(0, ITEMS, make, 0)
+    foreign_weights(level, targets.at[1], tables, high, low)
 
 
 def last_between_kernel(values, sources, targets, rows, cols, own, *rest):
@@ -243,7 +337,10 @@
 
 
 def later_kernel(level, pieces, own, high, low, out_hbm, current, left, stage, sems):
-    values = summed(level - 1, pieces, own)
+    if level == 1:
+        values = own[...] + pieces[...]
+    else:
+        values = summed(level - 1, pieces, own)
     current[...] = values
     stack_boxes(values[0], values[1], left)
     me = own_position(level)
@@ -289,6 +386,11 @@
 
 SENT = pltpu.HBM((4,) + FIELD, jnp.float32)
 KEPT = pltpu.VMEM(FIELD, jnp.float32)
+SPREAD = pltpu.VMEM((2, CHEB, NODES), jnp.float32)
+SMALL = pltpu.VMEM((2, CHEB, CHEB), jnp.float32)
+ONE = pltpu.VMEM((2 * NODES, NODES), jnp.bfloat16)
+PAIR = pltpu.VMEM((BOXES, 2 * NODES, NODES), jnp.bfloat16)
+COLUMNS = pltpu.VMEM((BOXES, NODES, 128), jnp.float32)
 MADE = pltpu.VMEM((ITEMS, 2 * NODES, NODES), jnp.bfloat16)
 
 
@@ -316,37 +418,48 @@
             far(interp_rows),
             far(interp_cols),
         )
+        packed, rows, cols = pl.pallas_call(
+            pack_kernel,
+            in_specs=[ANY] * 5,
+            out_specs=[WHOLE] * 3,
+            out_shape=[pltpu.VMEM((PACKED, NODES), jnp.float32), SMALL, SMALL],
+            scratch_shapes=(KEPT,) + node_buffers(None)[:2] + (pltpu.SemaphoreType.DMA((5,)),),
+            compiler_params=PARAMS,
+            name="pack",
+        )(far(current), *nodes)
+        got = swapped(packed, "sy")
+        partial, row0, col0 = pl.pallas_call(
+            near_kernel,
+            in_specs=[WHOLE] * 3,
+            out_specs=[WHOLE] * 3,
+            out_shape=[KEPT, SPREAD, SPREAD],
+            scratch_shapes=(COLUMNS, COLUMNS, PAIR, PAIR),
+            compiler_params=PARAMS,
+            cost_estimate=cost(20_000_000),
+            name="near",
+        )(packed, rows, cols)
         sent = pl.pallas_call(
-            first_kernel,
-            in_specs=[ANY] * 5,
-            out_specs=ANY,
-            out_shape=SENT,
-            scratch_shapes=(pltpu.VMEM(FIELD, jnp.float32),)
-            + node_buffers(None)
-            + TABLES
-            + (pltpu.VMEM((2, 2 * NODES, NODES), jnp.bfloat16),) * 2
-            + (LEFT, STAGE, pltpu.SemaphoreType.DMA((5,)), pltpu.SemaphoreType.DMA((FOREIGN,))),
+            partner_kernel,
+            in_specs=[WHOLE] * 4,
+            out_specs=WHOLE,
+            out_shape=KEPT,
+            scratch_shapes=(COLUMNS, COLUMNS, PAIR, PAIR),
             compiler_params=PARAMS,
-            name="first",
-        )(far(current), *nodes)
-        for level in range(1, LEVELS + 1):
-            last = level == LEVELS
-            made = pl.pallas_call(
-                last_between_kernel if last else functools.partial(between_kernel, level),
-                in_specs=[WHOLE] + [ANY] * 4,
-                out_specs=[WHOLE] * (1 if last else 3),
-                out_shape=[KEPT] + ([] if last else [MADE] * 2),
-                scratch_shapes=node_buffers(1 if last else 2)
-                + TABLES
-                + (pltpu.VMEM((2 * NODES, NODES), jnp.bfloat16),) * 2
-                + (LEFT, pltpu.SemaphoreType.DMA((4,))),
-                compiler_params=PARAMS,
-                cost_estimate=cost(60_000_000),
-                name=f"between_{level}",
-            )(current, *nodes)
-            pieces = exchange(sent, level - 1)
-            if last:
-                break
+            name="partner",
+        )(got, row0, col0, partial)
+        made = pl.pallas_call(
+            second_kernel,
+            in_specs=[WHOLE] * 4 + [ANY] * 4,
+            out_specs=[WHOLE] * 3,
+            out_shape=[KEPT, MADE, MADE],
+            scratch_shapes=node_buffers(None)
+            + (COLUMNS, COLUMNS, SPREAD, SPREAD, ONE, ONE, pltpu.SemaphoreType.DMA((4,))),
+            compiler_params=PARAMS,
+            cost_estimate=cost(60_000_000),
+            name="second",
+        )(packed, got, row0, col0, *nodes)
+        pieces = swapped(sent, "sx")
+        for level in range(1, LEVELS):
             sent, current = pl.pallas_call(
                 functools.partial(later_kernel, level),
                 in_specs=[WHOLE] * 4,
@@ -356,6 +469,20 @@
                 compiler_params=PARAMS,
                 name=f"later_{level}",
             )(pieces, *made)
+            last = level + 1 == LEVELS
+            made = pl.pallas_call(
+                last_between_kernel if last else functools.partial(between_kernel, level + 1),
+                in_specs=[WHOLE] + [ANY] * 4,
+                out_specs=[WHOLE] * (1 if last else 3),
+                out_shape=[KEPT] + ([] if last else [MADE] * 2),
+                scratch_shapes=node_buffers(1 if last else 2)
+                + TABLES
+                + (ONE, ONE, LEFT, pltpu.SemaphoreType.DMA((4,))),
+                compiler_params=PARAMS,
+                cost_estimate=cost(60_000_000),
+                name=f"between_{level + 1}",
+            )(current, *nodes)
+            pieces = exchange(sent, level)
         field = pl.pallas_call(
             final_kernel,
             in_specs=[WHOLE] * 2,

time: 44.2 us -> 43.1 us (0.975)
  the two profiles are of different devices: /device:TPU:2 before, /device:TPU:1 now
where the time goes in v1:
time: 43.1 us; the launch traced here: 42.6 us
  starting transfers between devices  19 us (44%)
  Pallas kernels  16.4 us (38%)
  waiting for transfers between devices  7.14 us (17%)
    ppermute x2, starting transfers between devices, swapped(): return lax.ppermute(block, axis, [(i, i ^ 1) for i in range(count)])  10.7 us
    all_to_all x2, starting transfers between devices, exchange(): lax.all_to_all(sent, ('sx', 'sy'), 0, 0, axis_index_groups=groups[level],...  8.29 us
    all_to_all x2, waiting for transfers between devices, exchange(): lax.all_to_all(sent, ('sx', 'sy'), 0, 0, axis_index_groups=groups[level],...  7.06 us
    pallas_call x2, Pallas kernels, local(): pl.pallas_call(last_between_kernel if last else functools.partial(between...  6.06 us
    pallas_call x1, Pallas kernels, local(): pl.pallas_call(second_kernel, in_specs=[WHOLE] * 4 + [ANY] * 4, out_specs...  4.54 us
    pallas_call x2, Pallas kernels, local(): pl.pallas_call(functools.partial(later_kernel, level), in_specs=[WHOLE] *...  2.58 us
    pallas_call x1, Pallas kernels, local(): pl.pallas_call(pack_kernel, in_specs=[ANY] * 5, out_specs=[WHOLE] * 3, ou...  0.9 us
  transfers between devices with their start and end apart: 4, of which 2 were waited for; matrix products, arithmetic and copies ran while one was open for 0% of the time, Pallas kernels for 27%

profile of v1, /device:TPU:1, one launch (start us, length us, event | category | flops | bytes accessed | tf_op | source)
XLA Modules:
  0.0 42.6 jit_solution(17152909976092357980)
XLA Ops:
  0.0 0.9 %pack.1 = (f32[88,256]{1,0:T(8,128)S(1)}, f32[2,16,16]{2,1,0:T(8,128)S(1)}, f32[2,16,16]{2,1,0:T(8,128)S(1)}) custom-call(f32[2,2,16,256]{3,2,1,0:T(8,128)} %bitcast.4, f32[3,2,2,1,256]{4,3,2,1,0:T(1,128)} %sources.1, f32[3,2,2,2,2,1,256]{6,5,4,3,2,1,0:T(1,128)} %targets.1, f32[3,2,16,16]{3,2,1,0:T(8,128)} %rows.1, f32[3,2,16,16]{3,2,1,0:T(8,128)} %cols.1), custom_call_target="tpu_custom_call" | custom-call | tf_op jit(solution)/shard_map/pack/pallas_call | solution.py:421
  0.9 8.7 %collective-permute-start = (f32[88,256]{1,0:T(8,128)S(1)}, f32[88,256]{1,0:T(8,128)S(1)}, u32[]{:S(2)}, u32[]{:S(2)}) collective-permute-start(f32[88,256]{1,0:T(8,128)S(1)} %get-tuple-element.21.packed), channel_id=1, source_target_pairs={{0,1},{1,0},{2,3},{3,2},{4,5},{5,4},{6,7},{7,6},{8,9},{9,8},{10,11... | collective-permute-start | bytes 270344 | tf_op jit(solution)/shard_map/ppermute | solution.py:50
  9.7 0.9 %near.1 = (f32[2,2,16,256]{3,2,1,0:T(8,128)S(1)}, f32[2,16,256]{2,1,0:T(8,128)S(1)}, f32[2,16,256]{2,1,0:T(8,128)S(1)}) custom-call(f32[88,256]{1,0:T(8,128)S(1)} %get-tuple-element.21.packed, f32[2,16,16]{2,1,0:T(8,128)S(1)} %get-tuple-element.22.rows, f32[2,16,16]{2,1,0:T(8,128)S(1)} %get-tuple-element.23.cols), custom_call_target="tpu_custom_call" | custom-call | flops 20000000 | bytes 100000 | tf_op jit(solution)/shard_map/near/pallas_call | solution.py:431
  10.5 0.0 collective-permute-done.packed.got
  10.6 0.9 %partner.1 = f32[2,2,16,256]{3,2,1,0:T(8,128)S(1)} custom-call(f32[88,256]{1,0:T(8,128)S(1)} %collective-permute-done.packed.got, f32[2,16,256]{2,1,0:T(8,128)S(1)} %get-tuple-element.24.row_ref.row0_ref, f32[2,16,256]{2,1,0:T(8,128)S(1)} %get-tuple-element.25.col_ref.col0_ref, f32[2,2,16,256]{3,2,1,0:T(8,128)S(1)} %get-tuple-element.26.partial), custom_call_target="tpu_custom_call" | custom-call | tf_op jit(solution)/shard_map/partner/pallas_call | solution.py:441
  11.4 1.9 %collective-permute-start.1 = (f32[2,2,16,256]{3,2,1,0:T(8,128)S(1)}, f32[2,2,16,256]{3,2,1,0:T(8,128)S(1)}, u32[]{:S(2)}, u32[]{:S(2)}) collective-permute-start(f32[2,2,16,256]{3,2,1,0:T(8,128)S(1)} %partner.1), channel_id=1, source_target_pairs={{0,32},{32,0},{64,96},{96,64},{128,160},{160,128},{192,224},{224,1... | collective-permute-start | bytes 196616 | tf_op jit(solution)/shard_map/ppermute | solution.py:50
  13.4 4.5 %second.1 = (f32[2,2,16,256]{3,2,1,0:T(8,128)S(1)}, bf16[6,512,256]{2,1,0:T(8,128)(2,1)S(1)}, bf16[6,512,256]{2,1,0:T(8,128)(2,1)S(1)}) custom-call(f32[88,256]{1,0:T(8,128)S(1)} %get-tuple-element.21.packed, f32[88,256]{1,0:T(8,128)S(1)} %collective-permute-done.packed.got, f32[2,16,256]{2,1,0:T(8,128)S(1)} %get-tuple-element.24.row_ref.row0_ref, ...), custom_call_target="tpu_custom_call" | custom-call | flops 60000000 | bytes 100000 | tf_op jit(solution)/shard_map/second/pallas_call | solution.py:450
  17.9 0.0 collective-permute-done.1.pieces
  18.0 1.3 %later_1.1 = (f32[4,2,2,16,256]{4,3,2,1,0:T(8,128)}, f32[2,2,16,256]{3,2,1,0:T(8,128)S(1)}) custom-call(f32[2,2,16,256]{3,2,1,0:T(8,128)S(1)} %collective-permute-done.1.pieces, f32[2,2,16,256]{3,2,1,0:T(8,128)S(1)} %get-tuple-element.27.own, bf16[6,512,256]{2,1,0:T(8,128)(2,1)S(1)} %get-tuple-element.28.high, bf16[6,512,256]{2,1,0:T(8,128)(2,1)S(1)} %get-tuple-element.29.low), custom_call_target="tpu_custom_call" | custom-call | tf_op jit(solution)/shard_map/later_1/pallas_call | solution.py:463
  19.3 3.4 %all-to-all-start = ((f32[4,2,2,16,256]{4,3,2,1,0:T(8,128)}), f32[4,2,2,16,256]{4,3,2,1,0:T(8,128)S(1)}, u32[]{:S(2)}, u32[]{:S(2)}) async-start(f32[4,2,2,16,256]{4,3,2,1,0:T(8,128)} %get-tuple-element.30), calls=%async_computation | async-start | bytes 524288 | tf_op jit(solution)/shard_map/all_to_all | solution.py:409
  22.7 4.1 %between_2.1 = (f32[2,2,16,256]{3,2,1,0:T(8,128)S(1)}, bf16[6,512,256]{2,1,0:T(8,128)(2,1)S(1)}, bf16[6,512,256]{2,1,0:T(8,128)(2,1)S(1)}) custom-call(f32[2,2,16,256]{3,2,1,0:T(8,128)S(1)} %get-tuple-element.31.values, f32[3,2,2,1,256]{4,3,2,1,0:T(1,128)} %sources.1, f32[3,2,2,2,2,1,256]{6,5,4,3,2,1,0:T(1,128)} %targets.1, f32[3,2,16,16]{3,2,1,0:T(8,128)} %rows.1, ...), custom_call_target="tpu_custom_call" | custom-call | flops 60000000 | bytes 100000 | tf_op jit(solution)/shard_map/between_2/pallas_call | solution.py:473
  26.8 0.1 all-to-all-done.pieces
  26.9 1.3 %later_2.1 = (f32[4,2,2,16,256]{4,3,2,1,0:T(8,128)}, f32[2,2,16,256]{3,2,1,0:T(8,128)S(1)}) custom-call(f32[4,2,2,16,256]{4,3,2,1,0:T(8,128)S(1)} %all-to-all-done.pieces, f32[2,2,16,256]{3,2,1,0:T(8,128)S(1)} %get-tuple-element.32.own, bf16[6,512,256]{2,1,0:T(8,128)(2,1)S(1)} %get-tuple-element.33.high, bf16[6,512,256]{2,1,0:T(8,128)(2,1)S(1)} %get-tuple-element.34.low), custom_call_target="tpu_custom_call" | custom-call | tf_op jit(solution)/shard_map/later_2/pallas_call | solution.py:463
  28.2 4.9 %all-to-all-start.1 = ((f32[4,2,2,16,256]{4,3,2,1,0:T(8,128)}), f32[4,2,2,16,256]{4,3,2,1,0:T(8,128)S(1)}, u32[]{:S(2)}, u32[]{:S(2)}) async-start(f32[4,2,2,16,256]{4,3,2,1,0:T(8,128)} %get-tuple-element.35), calls=%async_computation.1 | async-start | bytes 524288 | tf_op jit(solution)/shard_map/all_to_all | solution.py:409
  33.0 2.0 %between_3.1.own = f32[2,2,16,256]{3,2,1,0:T(8,128)S(1)} custom-call(f32[2,2,16,256]{3,2,1,0:T(8,128)S(1)} %get-tuple-element.36.values, f32[3,2,2,1,256]{4,3,2,1,0:T(1,128)} %sources.1, f32[3,2,2,2,2,1,256]{6,5,4,3,2,1,0:T(1,128)} %targets.1, f32[3,2,16,16]{3,2,1,0:T(8,128)} %rows.1, f32[3,2,16,16]{3,2,1,0:T(8,128)} %cols.1), custom_call_target="tpu_custom_call" | custom-call | flops 60000000 | bytes 100000 | tf_op jit(solution)/shard_map/between_3/pallas_call | solution.py:473
  35.0 7.0 %all-to-all-done.1.pieces = f32[4,2,2,16,256]{4,3,2,1,0:T(8,128)S(1)} async-done(((f32[4,2,2,16,256]{4,3,2,1,0:T(8,128)}), f32[4,2,2,16,256]{4,3,2,1,0:T(8,128)S(1)}, u32[]{:S(2)}, u32[]{:S(2)}) %all-to-all-start.1) | async-done | bytes 262176 | tf_op jit(solution)/shard_map/all_to_all | solution.py:409
  42.0 0.6 %final.1 = f32[2,2,16,256]{3,2,1,0:T(8,128)} custom-call(f32[4,2,2,16,256]{4,3,2,1,0:T(8,128)S(1)} %all-to-all-done.1.pieces, f32[2,2,16,256]{3,2,1,0:T(8,128)S(1)} %between_3.1.own), custom_call_target="tpu_custom_call" | custom-call | tf_op jit(solution)/shard_map/final/pallas_call | solution.py:486
Async XLA Ops:
  0.9 9.7 %collective-permute-start = (f32[88,256]{1,0:T(8,128)S(1)}, f32[88,256]{1,0:T(8,128)S(1)}, u32[]{:S(2)}, u32[]{:S(2)}) collective-permute-start(f32[88,256]{1,0:T(8,128)S(1)} %get-tuple-element.21.packed), channel_id=1, source_target_pairs={{0,1},{1,0},{2,3},{3,2},{4,5},{5,4},{6,7},{7,6},{8,9},{9,8},{10,11... | collective-permute-start | bytes 270344 | tf_op jit(solution)/shard_map/ppermute | solution.py:50
  11.4 6.5 %collective-permute-start.1 = (f32[2,2,16,256]{3,2,1,0:T(8,128)S(1)}, f32[2,2,16,256]{3,2,1,0:T(8,128)S(1)}, u32[]{:S(2)}, u32[]{:S(2)}) collective-permute-start(f32[2,2,16,256]{3,2,1,0:T(8,128)S(1)} %partner.1), channel_id=1, source_target_pairs={{0,32},{32,0},{64,96},{96,64},{128,160},{160,128},{192,224},{224,1... | collective-permute-start | bytes 196616 | tf_op jit(solution)/shard_map/ppermute | solution.py:50
  19.3 7.6 %all-to-all-start = ((f32[4,2,2,16,256]{4,3,2,1,0:T(8,128)}), f32[4,2,2,16,256]{4,3,2,1,0:T(8,128)S(1)}, u32[]{:S(2)}, u32[]{:S(2)}) async-start(f32[4,2,2,16,256]{4,3,2,1,0:T(8,128)} %get-tuple-element.30), calls=%async_computation | async-start | bytes 524288 | tf_op jit(solution)/shard_map/all_to_all | solution.py:409
  28.2 13.8 %all-to-all-start.1 = ((f32[4,2,2,16,256]{4,3,2,1,0:T(8,128)}), f32[4,2,2,16,256]{4,3,2,1,0:T(8,128)S(1)}, u32[]{:S(2)}, u32[]{:S(2)}) async-start(f32[4,2,2,16,256]{4,3,2,1,0:T(8,128)} %get-tuple-element.35), calls=%async_computation.1 | async-start | bytes 524288 | tf_op jit(solution)/shard_map/all_to_all | solution.py:409

commit v2 on v1

--- a/solution.py
+++ b/solution.py
@@ -20,6 +20,7 @@
 SOURCE_LINE = 2 * BOXES * RHS
 TARGET_LINE = SOURCE_LINE + 2 * BOXES
 PACKED = 88
+LOW_SCALE = 2.0**17
 
 
 def half_turn_coefficients():
@@ -133,7 +134,10 @@
         for where, value in ((down, real), (along, imag)):
             top = value.astype(jnp.bfloat16)
             high[where, :] = top
-            low[where, :] = (value - top.astype(jnp.float32)).astype(jnp.bfloat16)
+            rest_of = value - top.astype(jnp.float32)
+            if low.dtype != jnp.bfloat16:
+                rest_of = rest_of * LOW_SCALE
+            low[where, :] = rest_of.astype(low.dtype)
 
 
 def stacked(values):
@@ -154,7 +158,12 @@
 
 def product(left, high, low):
     main = jnp.dot(left, high, preferred_element_type=jnp.float32)
-    small = jnp.dot(left[: 2 * RHS], low, preferred_element_type=jnp.float32)
+    scaled = low.dtype != jnp.bfloat16
+    small = jnp.dot(
+        left[: 2 * RHS], low.astype(jnp.bfloat16), preferred_element_type=jnp.float32
+    )
+    if scaled:
+        small = small * (1.0 / LOW_SCALE)
     return main[: 2 * RHS] + main[2 * RHS :] + small
 
 
@@ -236,16 +245,21 @@
         sent[1, box] = partial[1, box] + both[box][RHS:]
 
 
-def foreign_weights(level, targets, tables, high, low):
+def make_weights(level, first, targets, tables, high, low):
     there = own_position(level)
 
     def make(item, carry):
         weigh(
-            there ^ (item // 2 + 1), item % 2, line_of(targets), tables, high.at[item], low.at[item]
+            there ^ (item // 2 + first),
+            item % 2,
+            line_of(targets),
+            tables,
+            high.at[item],
+            low.at[item],
         )
         return carry
 
-    lax.fori_loop(0, ITEMS, make, 0)
+    lax.fori_loop(0, (4 - first) * BOXES, make, 0)
 
 
 def second_kernel(
@@ -287,17 +301,15 @@
         copy.wait()
     tables = (a_ref, b_ref, row_ref, col_ref)
     prepare(sources, rows, cols, tables)
-    foreign_weights(1, targets, tables, high, low)
+    make_weights(1, 1, targets, tables, high, low)
 
 
 def between_kernel(
-    level, values, sources_hbm, targets_hbm, rows_hbm, cols_hbm, own, high, low,
+    values, sources_hbm, targets_hbm, rows_hbm, cols_hbm, own, high, low,
     sources, targets, rows, cols, *rest,
 ):
     *tables, own_high, own_low, left, sems = rest
-    last = level == LEVELS
-    count = 1 if last else 2
-    here = pl.ds(level - 1, count)
+    here = pl.ds(1, 2)
     nodes = fetch(
         [
             (sources_hbm.at[here], sources),
@@ -311,7 +323,7 @@
     for copy in nodes:
         copy.wait()
     prepare(sources.at[0], rows.at[0], cols.at[0], tables)
-    me = own_position(level - 1)
+    me = own_position(1)
 
     def mine(box, carry):
         weigh(me, box, line_of(targets.at[0]), tables, own_high, own_low)
@@ -321,29 +333,15 @@
         return carry
 
     lax.fori_loop(0, BOXES, mine, 0)
-    if last:
-        return
     prepare(sources.at[1], rows.at[1], cols.at[1], tables)
-    foreign_weights(level, targets.at[1], tables, high, low)
-
-
-def last_between_kernel(values, sources, targets, rows, cols, own, *rest):
-    between_kernel(LEVELS, values, sources, targets, rows, cols, own, None, None, *rest)
-
-
-def summed(level, pieces, own):
-    me = own_position(level)
-    return (own[...] + pieces[me ^ 1]) + (pieces[me ^ 2] + pieces[me ^ 3])
-
-
-def later_kernel(level, pieces, own, high, low, out_hbm, current, left, stage, sems):
-    if level == 1:
-        values = own[...] + pieces[...]
-    else:
-        values = summed(level - 1, pieces, own)
+    make_weights(2, 0, targets.at[1], tables, high, low)
+
+
+def middle_kernel(piece, own, high, low, out_hbm, current, left, stage, sems):
+    values = own[...] + piece[...]
     current[...] = values
     stack_boxes(values[0], values[1], left)
-    me = own_position(level)
+    me = own_position(1)
     sent = []
     for x in range(FOREIGN):
         for box in range(BOXES):
@@ -356,8 +354,19 @@
         copy.wait()
 
 
-def final_kernel(pieces, own, out):
-    out[...] = summed(LEVELS - 1, pieces, own)
+def late_kernel(pieces, own, high, low, out, left):
+    me = own_position(1)
+    values = (own[...] + pieces[me ^ 1]) + (pieces[me ^ 2] + pieces[me ^ 3])
+    stack_boxes(values[0], values[1], left)
+    there = own_position(2)
+    for x in range(4):
+        for box in range(BOXES):
+            item = 2 * x + box
+            put(out, there ^ x, box, product(left[box], high[item], low[item]))
+
+
+def final_kernel(pieces, out):
+    out[...] = (pieces[0] + pieces[1]) + (pieces[2] + pieces[3])
 
 
 def node_buffers(count):
@@ -459,38 +468,47 @@
             name="second",
         )(packed, got, row0, col0, *nodes)
         pieces = swapped(sent, "sx")
-        for level in range(1, LEVELS):
-            sent, current = pl.pallas_call(
-                functools.partial(later_kernel, level),
-                in_specs=[WHOLE] * 4,
-                out_specs=[ANY, WHOLE],
-                out_shape=[SENT, KEPT],
-                scratch_shapes=(LEFT, STAGE, pltpu.SemaphoreType.DMA((FOREIGN,))),
-                compiler_params=PARAMS,
-                name=f"later_{level}",
-            )(pieces, *made)
-            last = level + 1 == LEVELS
-            made = pl.pallas_call(
-                last_between_kernel if last else functools.partial(between_kernel, level + 1),
-                in_specs=[WHOLE] + [ANY] * 4,
-                out_specs=[WHOLE] * (1 if last else 3),
-                out_shape=[KEPT] + ([] if last else [MADE] * 2),
-                scratch_shapes=node_buffers(1 if last else 2)
-                + TABLES
-                + (ONE, ONE, LEFT, pltpu.SemaphoreType.DMA((4,))),
-                compiler_params=PARAMS,
-                cost_estimate=cost(60_000_000),
-                name=f"between_{level + 1}",
-            )(current, *nodes)
-            pieces = exchange(sent, level)
+        sent, current = pl.pallas_call(
+            middle_kernel,
+            in_specs=[WHOLE] * 4,
+            out_specs=[ANY, WHOLE],
+            out_shape=[SENT, KEPT],
+            scratch_shapes=(LEFT, STAGE, pltpu.SemaphoreType.DMA((FOREIGN,))),
+            compiler_params=PARAMS,
+            name="middle",
+        )(pieces, *made)
+        made = pl.pallas_call(
+            between_kernel,
+            in_specs=[WHOLE] + [ANY] * 4,
+            out_specs=[WHOLE] * 3,
+            out_shape=[
+                KEPT,
+                pltpu.VMEM((4 * BOXES, 2 * NODES, NODES), jnp.bfloat16),
+                pltpu.VMEM((4 * BOXES, 2 * NODES, NODES), jnp.float8_e4m3fn),
+            ],
+            scratch_shapes=node_buffers(2) + TABLES + (ONE, ONE, LEFT, pltpu.SemaphoreType.DMA((4,))),
+            compiler_params=PARAMS,
+            cost_estimate=cost(60_000_000),
+            name="between",
+        )(current, *nodes)
+        pieces = exchange(sent, 1)
+        sent = pl.pallas_call(
+            late_kernel,
+            in_specs=[WHOLE] * 4,
+            out_specs=WHOLE,
+            out_shape=pltpu.VMEM((4,) + FIELD, jnp.float32),
+            scratch_shapes=(LEFT,),
+            compiler_params=PARAMS,
+            name="late",
+        )(pieces, *made)
         field = pl.pallas_call(
             final_kernel,
-            in_specs=[WHOLE] * 2,
+            in_specs=[WHOLE],
             out_specs=WHOLE,
             out_shape=jax.ShapeDtypeStruct(FIELD, jnp.float32),
             compiler_params=PARAMS,
             name="final",
-        )(pieces, *made)
+        )(exchange(sent, 2))
         return field.reshape(2, BOXES, 1, RHS, NODES)
 
     in_specs = (

time: 43.1 us -> 41.9 us (0.972)
  the two profiles are of different devices: /device:TPU:1 before, /device:TPU:16 now
where the time goes in v2:
time: 41.9 us; the launch traced here: 41.5 us
  Pallas kernels  14.8 us (35%)
  blocking collectives  14.8 us (35%)
  starting transfers between devices  10.6 us (25%)
  waiting for transfers between devices  1.32 us (3%)
    all_to_all x1, blocking collectives, exchange(): lax.all_to_all(sent, ('sx', 'sy'), 0, 0, axis_index_groups=groups[level],...  14.8 us
    ppermute x2, starting transfers between devices, swapped(): return lax.ppermute(block, axis, [(i, i ^ 1) for i in range(count)])  6.85 us
    pallas_call x1, Pallas kernels, local(): pl.pallas_call(between_kernel, in_specs=[WHOLE] + [ANY] * 4, out_specs=[W...  4.89 us
    pallas_call x1, Pallas kernels, local(): pl.pallas_call(second_kernel, in_specs=[WHOLE] * 4 + [ANY] * 4, out_specs...  4.55 us
    all_to_all x1, starting transfers between devices, exchange(): lax.all_to_all(sent, ('sx', 'sy'), 0, 0, axis_index_groups=groups[level],...  3.7 us
    pallas_call x1, Pallas kernels, local(): pl.pallas_call(middle_kernel, in_specs=[WHOLE] * 4, out_specs=[ANY, WHOLE...  1.29 us
    all_to_all x1, waiting for transfers between devices, exchange(): lax.all_to_all(sent, ('sx', 'sy'), 0, 0, axis_index_groups=groups[level],...  0.93 us
    pallas_call x1, Pallas kernels, local(): pl.pallas_call(pack_kernel, in_specs=[ANY] * 5, out_specs=[WHOLE] * 3, ou...  0.9 us
  transfers between devices with their start and end apart: 3, of which 2 were waited for; matrix products, arithmetic and copies ran while one was open for 0% of the time, Pallas kernels for 25%

profile of v2, /device:TPU:16, one launch (start us, length us, event | category | flops | bytes accessed | tf_op | source)
XLA Modules:
  0.0 41.5 jit_solution(6393921097469498573)
XLA Ops:
  0.0 0.9 %pack.1 = (f32[88,256]{1,0:T(8,128)S(1)}, f32[2,16,16]{2,1,0:T(8,128)S(1)}, f32[2,16,16]{2,1,0:T(8,128)S(1)}) custom-call(f32[2,2,16,256]{3,2,1,0:T(8,128)} %bitcast.4, f32[3,2,2,1,256]{4,3,2,1,0:T(1,128)} %sources_hbm.5, f32[3,2,2,2,2,1,256]{6,5,4,3,2,1,0:T(1,128)} %targets_hbm.5, f32[3,2,16,16]{3,2,1,0:T(8,128)} %rows_hbm.5, f32[3,2,16,16]{3,2,1,0:T(8,128)} %cols_hbm.5), custom_call_target="tpu_custom_call" | custom-call | tf_op jit(solution)/shard_map/pack/pallas_call | solution.py:430
  0.9 1.9 %collective-permute-start = (f32[88,256]{1,0:T(8,128)S(1)}, f32[88,256]{1,0:T(8,128)S(1)}, u32[]{:S(2)}, u32[]{:S(2)}) collective-permute-start(f32[88,256]{1,0:T(8,128)S(1)} %get-tuple-element.19.packed), channel_id=1, source_target_pairs={{0,1},{1,0},{2,3},{3,2},{4,5},{5,4},{6,7},{7,6},{8,9},{9,8},{10,11... | collective-permute-start | bytes 270344 | tf_op jit(solution)/shard_map/ppermute | solution.py:51
  2.8 0.9 %near.1 = (f32[2,2,16,256]{3,2,1,0:T(8,128)S(1)}, f32[2,16,256]{2,1,0:T(8,128)S(1)}, f32[2,16,256]{2,1,0:T(8,128)S(1)}) custom-call(f32[88,256]{1,0:T(8,128)S(1)} %get-tuple-element.19.packed, f32[2,16,16]{2,1,0:T(8,128)S(1)} %get-tuple-element.20.rows, f32[2,16,16]{2,1,0:T(8,128)S(1)} %get-tuple-element.21.cols), custom_call_target="tpu_custom_call" | custom-call | flops 20000000 | bytes 100000 | tf_op jit(solution)/shard_map/near/pallas_call | solution.py:440
  3.7 0.4 collective-permute-done.packed.got
  4.1 0.9 %partner.1 = f32[2,2,16,256]{3,2,1,0:T(8,128)S(1)} custom-call(f32[88,256]{1,0:T(8,128)S(1)} %collective-permute-done.packed.got, f32[2,16,256]{2,1,0:T(8,128)S(1)} %get-tuple-element.22.row_ref.row0_ref, f32[2,16,256]{2,1,0:T(8,128)S(1)} %get-tuple-element.23.col_ref.col0_ref, f32[2,2,16,256]{3,2,1,0:T(8,128)S(1)} %get-tuple-element.24.partial), custom_call_target="tpu_custom_call" | custom-call | tf_op jit(solution)/shard_map/partner/pallas_call | solution.py:450
  5.0 4.9 %collective-permute-start.1 = (f32[2,2,16,256]{3,2,1,0:T(8,128)S(1)}, f32[2,2,16,256]{3,2,1,0:T(8,128)S(1)}, u32[]{:S(2)}, u32[]{:S(2)}) collective-permute-start(f32[2,2,16,256]{3,2,1,0:T(8,128)S(1)} %partner.1), channel_id=1, source_target_pairs={{0,32},{32,0},{64,96},{96,64},{128,160},{160,128},{192,224},{224,1... | collective-permute-start | bytes 196616 | tf_op jit(solution)/shard_map/ppermute | solution.py:51
  9.9 4.5 %second.1 = (f32[2,2,16,256]{3,2,1,0:T(8,128)S(1)}, bf16[6,512,256]{2,1,0:T(8,128)(2,1)S(1)}, bf16[6,512,256]{2,1,0:T(8,128)(2,1)S(1)}) custom-call(f32[88,256]{1,0:T(8,128)S(1)} %get-tuple-element.19.packed, f32[88,256]{1,0:T(8,128)S(1)} %collective-permute-done.packed.got, f32[2,16,256]{2,1,0:T(8,128)S(1)} %get-tuple-element.22.row_ref.row0_ref, ...), custom_call_target="tpu_custom_call" | custom-call | flops 60000000 | bytes 100000 | tf_op jit(solution)/shard_map/second/pallas_call | solution.py:459
  14.5 0.0 collective-permute-done.1.piece
  14.5 1.3 %middle.1 = (f32[4,2,2,16,256]{4,3,2,1,0:T(8,128)}, f32[2,2,16,256]{3,2,1,0:T(8,128)S(1)}) custom-call(f32[2,2,16,256]{3,2,1,0:T(8,128)S(1)} %collective-permute-done.1.piece, f32[2,2,16,256]{3,2,1,0:T(8,128)S(1)} %get-tuple-element.25.own, bf16[6,512,256]{2,1,0:T(8,128)(2,1)S(1)} %get-tuple-element.26.high, bf16[6,512,256]{2,1,0:T(8,128)(2,1)S(1)} %get-tuple-element.27.low), custom_call_target="tpu_custom_call" | custom-call | tf_op jit(solution)/shard_map/middle/pallas_call | solution.py:471
  15.8 3.7 %all-to-all-start = ((f32[4,2,2,16,256]{4,3,2,1,0:T(8,128)}), f32[4,2,2,16,256]{4,3,2,1,0:T(8,128)S(1)}, u32[]{:S(2)}, u32[]{:S(2)}) async-start(f32[4,2,2,16,256]{4,3,2,1,0:T(8,128)} %get-tuple-element.28), calls=%async_computation | async-start | bytes 524288 | tf_op jit(solution)/shard_map/all_to_all | solution.py:418
  19.5 4.9 %between.1 = (f32[2,2,16,256]{3,2,1,0:T(8,128)S(1)}, bf16[8,512,256]{2,1,0:T(8,128)(2,1)S(1)}, f8e4m3fn[8,512,256]{2,1,0:T(32,128)(4,1)S(1)}) custom-call(f32[2,2,16,256]{3,2,1,0:T(8,128)S(1)} %get-tuple-element.29.values, f32[3,2,2,1,256]{4,3,2,1,0:T(1,128)} %sources_hbm.5, f32[3,2,2,2,2,1,256]{6,5,4,3,2,1,0:T(1,128)} %targets_hbm.5, ...), custom_call_target="tpu_custom_call" | custom-call | flops 60000000 | bytes 100000 | tf_op jit(solution)/shard_map/between/pallas_call | solution.py:480
  24.4 0.9 %all-to-all-done.pieces = f32[4,2,2,16,256]{4,3,2,1,0:T(8,128)S(1)} async-done(((f32[4,2,2,16,256]{4,3,2,1,0:T(8,128)}), f32[4,2,2,16,256]{4,3,2,1,0:T(8,128)S(1)}, u32[]{:S(2)}, u32[]{:S(2)}) %all-to-all-start) | async-done | bytes 262176 | tf_op jit(solution)/shard_map/all_to_all | solution.py:418
  25.3 0.8 %late.1 = f32[4,2,2,16,256]{4,3,2,1,0:T(8,128)S(1)} custom-call(f32[4,2,2,16,256]{4,3,2,1,0:T(8,128)S(1)} %all-to-all-done.pieces, f32[2,2,16,256]{3,2,1,0:T(8,128)S(1)} %get-tuple-element.30.own, bf16[8,512,256]{2,1,0:T(8,128)(2,1)S(1)} %get-tuple-element.31.high, f8e4m3fn[8,512,256]{2,1,0:T(32,128)(4,1)S(1)} %get-tuple-element.32.low), custom_call_target="tpu_custom_call" | custom-call | tf_op jit(solution)/shard_map/late/pallas_call | solution.py:495
  26.1 14.8 %all_to_all.10.pieces = f32[4,2,2,16,256]{4,3,2,1,0:T(8,128)S(1)} all-to-all(f32[4,2,2,16,256]{4,3,2,1,0:T(8,128)S(1)} %late.1), channel_id=1, replica_groups={{0,4,128,132},{1,5,129,133},{2,6,130,134},{3,7,131,135},{8,12,136,140},..., dimensions={0} | all-to-all | bytes 524288 | tf_op jit(solution)/shard_map/all_to_all | solution.py:418
  40.9 0.6 %final.1 = f32[2,2,16,256]{3,2,1,0:T(8,128)} custom-call(f32[4,2,2,16,256]{4,3,2,1,0:T(8,128)S(1)} %all_to_all.10.pieces), custom_call_target="tpu_custom_call" | custom-call | tf_op jit(solution)/shard_map/final/pallas_call | solution.py:504
Async XLA Ops:
  0.9 3.2 %collective-permute-start = (f32[88,256]{1,0:T(8,128)S(1)}, f32[88,256]{1,0:T(8,128)S(1)}, u32[]{:S(2)}, u32[]{:S(2)}) collective-permute-start(f32[88,256]{1,0:T(8,128)S(1)} %get-tuple-element.19.packed), channel_id=1, source_target_pairs={{0,1},{1,0},{2,3},{3,2},{4,5},{5,4},{6,7},{7,6},{8,9},{9,8},{10,11... | collective-permute-start | bytes 270344 | tf_op jit(solution)/shard_map/ppermute | solution.py:51
  5.0 9.5 %collective-permute-start.1 = (f32[2,2,16,256]{3,2,1,0:T(8,128)S(1)}, f32[2,2,16,256]{3,2,1,0:T(8,128)S(1)}, u32[]{:S(2)}, u32[]{:S(2)}) collective-permute-start(f32[2,2,16,256]{3,2,1,0:T(8,128)S(1)} %partner.1), channel_id=1, source_target_pairs={{0,32},{32,0},{64,96},{96,64},{128,160},{160,128},{192,224},{224,1... | collective-permute-start | bytes 196616 | tf_op jit(solution)/shard_map/ppermute | solution.py:51
  15.8 9.5 %all-to-all-start = ((f32[4,2,2,16,256]{4,3,2,1,0:T(8,128)}), f32[4,2,2,16,256]{4,3,2,1,0:T(8,128)S(1)}, u32[]{:S(2)}, u32[]{:S(2)}) async-start(f32[4,2,2,16,256]{4,3,2,1,0:T(8,128)} %get-tuple-element.28), calls=%async_computation | async-start | bytes 524288 | tf_op jit(solution)/shard_map/all_to_all | solution.py:418

commit v3 on v2

--- a/solution.py
+++ b/solution.py
@@ -79,6 +79,15 @@
     for bit in range(2):
         row_ref[bit] = spread(rows[bit], outer)
         col_ref[bit] = spread(cols[bit], inner)
+
+
+def normalize(matrices, normal, level):
+    for bit in range(2):
+        values = matrices[bit]
+        top = jnp.max(jnp.abs(values), axis=(0, 1), keepdims=True)
+        safe = jnp.where(top > 0.0, top, 1.0)
+        normal[bit] = values / safe
+        level[pl.ds(bit, 1), :] = jnp.broadcast_to(safe, (1, 128))
 
 
 def spread_sources(source, a_ref, b_ref):
@@ -160,7 +169,7 @@
     main = jnp.dot(left, high, preferred_element_type=jnp.float32)
     scaled = low.dtype != jnp.bfloat16
     small = jnp.dot(
-        left[: 2 * RHS], low.astype(jnp.bfloat16), preferred_element_type=jnp.float32
+        left[: 2 * RHS], low, preferred_element_type=jnp.float32
     )
     if scaled:
         small = small * (1.0 / LOW_SCALE)
@@ -305,10 +314,10 @@
 
 
 def between_kernel(
-    values, sources_hbm, targets_hbm, rows_hbm, cols_hbm, own, high, low,
+    values, sources_hbm, targets_hbm, rows_hbm, cols_hbm, own, high, low, row_size, col_size,
     sources, targets, rows, cols, *rest,
 ):
-    *tables, own_high, own_low, left, sems = rest
+    *tables, own_high, own_low, left, row_normal, col_normal, sems = rest
     here = pl.ds(1, 2)
     nodes = fetch(
         [
@@ -333,7 +342,9 @@
         return carry
 
     lax.fori_loop(0, BOXES, mine, 0)
-    prepare(sources.at[1], rows.at[1], cols.at[1], tables)
+    normalize(rows.at[1], row_normal, row_size)
+    normalize(cols.at[1], col_normal, col_size)
+    prepare(sources.at[1], row_normal, col_normal, tables)
     make_weights(2, 0, targets.at[1], tables, high, low)
 
 
@@ -354,15 +365,18 @@
         copy.wait()
 
 
-def late_kernel(pieces, own, high, low, out, left):
+def late_kernel(pieces, own, high, low, row_size, col_size, out, left):
     me = own_position(1)
     values = (own[...] + pieces[me ^ 1]) + (pieces[me ^ 2] + pieces[me ^ 3])
     stack_boxes(values[0], values[1], left)
     there = own_position(2)
     for x in range(4):
+        place = there ^ x
+        size = row_size[pl.ds(place // 2, 1), :] * col_size[pl.ds(place % 2, 1), :]
+        size = jnp.concatenate([size, size], axis=1)
         for box in range(BOXES):
             item = 2 * x + box
-            put(out, there ^ x, box, product(left[box], high[item], low[item]))
+            put(out, place, box, product(left[box], high[item], low[item]) * size)
 
 
 def final_kernel(pieces, out):
@@ -480,13 +494,17 @@
         made = pl.pallas_call(
             between_kernel,
             in_specs=[WHOLE] + [ANY] * 4,
-            out_specs=[WHOLE] * 3,
+            out_specs=[WHOLE] * 5,
             out_shape=[
                 KEPT,
                 pltpu.VMEM((4 * BOXES, 2 * NODES, NODES), jnp.bfloat16),
                 pltpu.VMEM((4 * BOXES, 2 * NODES, NODES), jnp.float8_e4m3fn),
+                pltpu.VMEM((2, 128), jnp.float32),
+                pltpu.VMEM((2, 128), jnp.float32),
             ],
-            scratch_shapes=node_buffers(2) + TABLES + (ONE, ONE, LEFT, pltpu.SemaphoreType.DMA((4,))),
+            scratch_shapes=node_buffers(2)
+            + TABLES
+            + (ONE, ONE, LEFT, SMALL, SMALL, pltpu.SemaphoreType.DMA((4,))),
             compiler_params=PARAMS,
             cost_estimate=cost(60_000_000),
             name="between",
@@ -494,7 +512,7 @@
         pieces = exchange(sent, 1)
         sent = pl.pallas_call(
             late_kernel,
-            in_specs=[WHOLE] * 4,
+            in_specs=[WHOLE] * 6,
             out_specs=WHOLE,
             out_shape=pltpu.VMEM((4,) + FIELD, jnp.float32),
             scratch_shapes=(LEFT,),

time: 41.9 us -> 41.9 us (level)
  no operation moved by 1% of the time
where the time goes in v3:
time: 41.9 us; the launch traced here: 41.5 us
  blocking collectives  15 us (36%)
  Pallas kernels  14.8 us (35%)
  starting transfers between devices  10.6 us (25%)
  waiting for transfers between devices  1.11 us (3%)
    all_to_all x1, blocking collectives, exchange(): lax.all_to_all(sent, ('sx', 'sy'), 0, 0, axis_index_groups=groups[level],...  15 us
    ppermute x2, starting transfers between devices, swapped(): return lax.ppermute(block, axis, [(i, i ^ 1) for i in range(count)])  6.85 us
    pallas_call x1, Pallas kernels, local(): pl.pallas_call(between_kernel, in_specs=[WHOLE] + [ANY] * 4, out_specs=[W...  5.1 us
    pallas_call x1, Pallas kernels, local(): pl.pallas_call(second_kernel, in_specs=[WHOLE] * 4 + [ANY] * 4, out_specs...  4.55 us
    all_to_all x1, starting transfers between devices, exchange(): lax.all_to_all(sent, ('sx', 'sy'), 0, 0, axis_index_groups=groups[level],...  3.7 us
    pallas_call x1, Pallas kernels, local(): pl.pallas_call(middle_kernel, in_specs=[WHOLE] * 4, out_specs=[ANY, WHOLE...  1.29 us
    pallas_call x1, Pallas kernels, local(): pl.pallas_call(pack_kernel, in_specs=[ANY] * 5, out_specs=[WHOLE] * 3, ou...  0.9 us
    pallas_call x1, Pallas kernels, local(): pl.pallas_call(near_kernel, in_specs=[WHOLE] * 3, out_specs=[WHOLE] * 3,...  0.86 us
  transfers between devices with their start and end apart: 3, of which 2 were waited for; matrix products, arithmetic and copies ran while one was open for 0% of the time, Pallas kernels for 25%

profile of v3, /device:TPU:16, one launch (start us, length us, event | category | flops | bytes accessed | tf_op | source)
XLA Modules:
  0.0 41.5 jit_solution(10223118101570449683)
XLA Ops:
  0.0 0.9 %pack.1 = (f32[88,256]{1,0:T(8,128)S(1)}, f32[2,16,16]{2,1,0:T(8,128)S(1)}, f32[2,16,16]{2,1,0:T(8,128)S(1)}) custom-call(f32[2,2,16,256]{3,2,1,0:T(8,128)} %bitcast.4, f32[3,2,2,1,256]{4,3,2,1,0:T(1,128)} %sources_hbm.5, f32[3,2,2,2,2,1,256]{6,5,4,3,2,1,0:T(1,128)} %targets_hbm.5, f32[3,2,16,16]{3,2,1,0:T(8,128)} %rows_hbm.5, f32[3,2,16,16]{3,2,1,0:T(8,128)} %cols_hbm.5), custom_call_target="tpu_custom_call" | custom-call | tf_op jit(solution)/shard_map/pack/pallas_call | solution.py:444
  0.9 1.9 %collective-permute-start = (f32[88,256]{1,0:T(8,128)S(1)}, f32[88,256]{1,0:T(8,128)S(1)}, u32[]{:S(2)}, u32[]{:S(2)}) collective-permute-start(f32[88,256]{1,0:T(8,128)S(1)} %get-tuple-element.21.packed), channel_id=1, source_target_pairs={{0,1},{1,0},{2,3},{3,2},{4,5},{5,4},{6,7},{7,6},{8,9},{9,8},{10,11... | collective-permute-start | bytes 270344 | tf_op jit(solution)/shard_map/ppermute | solution.py:51
  2.8 0.9 %near.1 = (f32[2,2,16,256]{3,2,1,0:T(8,128)S(1)}, f32[2,16,256]{2,1,0:T(8,128)S(1)}, f32[2,16,256]{2,1,0:T(8,128)S(1)}) custom-call(f32[88,256]{1,0:T(8,128)S(1)} %get-tuple-element.21.packed, f32[2,16,16]{2,1,0:T(8,128)S(1)} %get-tuple-element.22.rows, f32[2,16,16]{2,1,0:T(8,128)S(1)} %get-tuple-element.23.cols), custom_call_target="tpu_custom_call" | custom-call | flops 20000000 | bytes 100000 | tf_op jit(solution)/shard_map/near/pallas_call | solution.py:454
  3.7 0.4 collective-permute-done.packed.got
  4.1 0.9 %partner.1 = f32[2,2,16,256]{3,2,1,0:T(8,128)S(1)} custom-call(f32[88,256]{1,0:T(8,128)S(1)} %collective-permute-done.packed.got, f32[2,16,256]{2,1,0:T(8,128)S(1)} %get-tuple-element.24.row_ref.row0_ref, f32[2,16,256]{2,1,0:T(8,128)S(1)} %get-tuple-element.25.col_ref.col0_ref, f32[2,2,16,256]{3,2,1,0:T(8,128)S(1)} %get-tuple-element.26.partial), custom_call_target="tpu_custom_call" | custom-call | tf_op jit(solution)/shard_map/partner/pallas_call | solution.py:464
  5.0 4.9 %collective-permute-start.1 = (f32[2,2,16,256]{3,2,1,0:T(8,128)S(1)}, f32[2,2,16,256]{3,2,1,0:T(8,128)S(1)}, u32[]{:S(2)}, u32[]{:S(2)}) collective-permute-start(f32[2,2,16,256]{3,2,1,0:T(8,128)S(1)} %partner.1), channel_id=1, source_target_pairs={{0,32},{32,0},{64,96},{96,64},{128,160},{160,128},{192,224},{224,1... | collective-permute-start | bytes 196616 | tf_op jit(solution)/shard_map/ppermute | solution.py:51
  9.9 4.5 %second.1 = (f32[2,2,16,256]{3,2,1,0:T(8,128)S(1)}, bf16[6,512,256]{2,1,0:T(8,128)(2,1)S(1)}, bf16[6,512,256]{2,1,0:T(8,128)(2,1)S(1)}) custom-call(f32[88,256]{1,0:T(8,128)S(1)} %get-tuple-element.21.packed, f32[88,256]{1,0:T(8,128)S(1)} %collective-permute-done.packed.got, f32[2,16,256]{2,1,0:T(8,128)S(1)} %get-tuple-element.24.row_ref.row0_ref, ...), custom_call_target="tpu_custom_call" | custom-call | flops 60000000 | bytes 100000 | tf_op jit(solution)/shard_map/second/pallas_call | solution.py:473
  14.5 0.0 collective-permute-done.1.piece
  14.5 1.3 %middle.1 = (f32[4,2,2,16,256]{4,3,2,1,0:T(8,128)}, f32[2,2,16,256]{3,2,1,0:T(8,128)S(1)}) custom-call(f32[2,2,16,256]{3,2,1,0:T(8,128)S(1)} %collective-permute-done.1.piece, f32[2,2,16,256]{3,2,1,0:T(8,128)S(1)} %get-tuple-element.27.own, bf16[6,512,256]{2,1,0:T(8,128)(2,1)S(1)} %get-tuple-element.28.high, bf16[6,512,256]{2,1,0:T(8,128)(2,1)S(1)} %get-tuple-element.29.low), custom_call_target="tpu_custom_call" | custom-call | tf_op jit(solution)/shard_map/middle/pallas_call | solution.py:485
  15.8 3.7 %all-to-all-start = ((f32[4,2,2,16,256]{4,3,2,1,0:T(8,128)}), f32[4,2,2,16,256]{4,3,2,1,0:T(8,128)S(1)}, u32[]{:S(2)}, u32[]{:S(2)}) async-start(f32[4,2,2,16,256]{4,3,2,1,0:T(8,128)} %get-tuple-element.30), calls=%async_computation | async-start | bytes 524288 | tf_op jit(solution)/shard_map/all_to_all | solution.py:432
  19.5 5.1 %between.1 = (f32[2,2,16,256]{3,2,1,0:T(8,128)S(1)}, bf16[8,512,256]{2,1,0:T(8,128)(2,1)S(1)}, f8e4m3fn[8,512,256]{2,1,0:T(32,128)(4,1)S(1)}, f32[2,128]{1,0:T(2,128)S(1)}, f32[2,128]{1,0:T(2,128)S(1)}) custom-call(f32[2,2,16,256]{3,2,1,0:T(8,128)S(1)} %get-tuple-element.31.values, f32[3,2,2,1,256]{4,3,2,1,0:T(1,128)} %sources_hbm.5, ...), custom_call_target="tpu_custom_call" | custom-call | flops 60000000 | bytes 100000 | tf_op jit(solution)/shard_map/between/pallas_call | solution.py:494
  24.6 0.7 %all-to-all-done.pieces = f32[4,2,2,16,256]{4,3,2,1,0:T(8,128)S(1)} async-done(((f32[4,2,2,16,256]{4,3,2,1,0:T(8,128)}), f32[4,2,2,16,256]{4,3,2,1,0:T(8,128)S(1)}, u32[]{:S(2)}, u32[]{:S(2)}) %all-to-all-start) | async-done | bytes 262176 | tf_op jit(solution)/shard_map/all_to_all | solution.py:432
  25.3 0.6 %late.1 = f32[4,2,2,16,256]{4,3,2,1,0:T(8,128)S(1)} custom-call(f32[4,2,2,16,256]{4,3,2,1,0:T(8,128)S(1)} %all-to-all-done.pieces, f32[2,2,16,256]{3,2,1,0:T(8,128)S(1)} %get-tuple-element.32.own, bf16[8,512,256]{2,1,0:T(8,128)(2,1)S(1)} %get-tuple-element.33.high, f8e4m3fn[8,512,256]{2,1,0:T(32,128)(4,1)S(1)} %get-tuple-element.34.low, ...), custom_call_target="tpu_custom_call" | custom-call | tf_op jit(solution)/shard_map/late/pallas_call | solution.py:513
  25.9 15.0 %all_to_all.10.pieces = f32[4,2,2,16,256]{4,3,2,1,0:T(8,128)S(1)} all-to-all(f32[4,2,2,16,256]{4,3,2,1,0:T(8,128)S(1)} %late.1), channel_id=1, replica_groups={{0,4,128,132},{1,5,129,133},{2,6,130,134},{3,7,131,135},{8,12,136,140},..., dimensions={0} | all-to-all | bytes 524288 | tf_op jit(solution)/shard_map/all_to_all | solution.py:432
  40.8 0.6 %final.1 = f32[2,2,16,256]{3,2,1,0:T(8,128)} custom-call(f32[4,2,2,16,256]{4,3,2,1,0:T(8,128)S(1)} %all_to_all.10.pieces), custom_call_target="tpu_custom_call" | custom-call | tf_op jit(solution)/shard_map/final/pallas_call | solution.py:522
Async XLA Ops:
  0.9 3.2 %collective-permute-start = (f32[88,256]{1,0:T(8,128)S(1)}, f32[88,256]{1,0:T(8,128)S(1)}, u32[]{:S(2)}, u32[]{:S(2)}) collective-permute-start(f32[88,256]{1,0:T(8,128)S(1)} %get-tuple-element.21.packed), channel_id=1, source_target_pairs={{0,1},{1,0},{2,3},{3,2},{4,5},{5,4},{6,7},{7,6},{8,9},{9,8},{10,11... | collective-permute-start | bytes 270344 | tf_op jit(solution)/shard_map/ppermute | solution.py:51
  5.0 9.5 %collective-permute-start.1 = (f32[2,2,16,256]{3,2,1,0:T(8,128)S(1)}, f32[2,2,16,256]{3,2,1,0:T(8,128)S(1)}, u32[]{:S(2)}, u32[]{:S(2)}) collective-permute-start(f32[2,2,16,256]{3,2,1,0:T(8,128)S(1)} %partner.1), channel_id=1, source_target_pairs={{0,32},{32,0},{64,96},{96,64},{128,160},{160,128},{192,224},{224,1... | collective-permute-start | bytes 196616 | tf_op jit(solution)/shard_map/ppermute | solution.py:51
  15.8 9.5 %all-to-all-start = ((f32[4,2,2,16,256]{4,3,2,1,0:T(8,128)}), f32[4,2,2,16,256]{4,3,2,1,0:T(8,128)S(1)}, u32[]{:S(2)}, u32[]{:S(2)}) async-start(f32[4,2,2,16,256]{4,3,2,1,0:T(8,128)} %get-tuple-element.30), calls=%async_computation | async-start | bytes 524288 | tf_op jit(solution)/shard_map/all_to_all | solution.py:432

commit v4 on v3

--- a/solution.py
+++ b/solution.py
@@ -272,10 +272,11 @@
 
 
 def second_kernel(
-    packed, got, row0_ref, col0_ref, sources_hbm, targets_hbm, rows_hbm, cols_hbm, own, high, low,
-    sources, targets, rows, cols, *rest,
+    packed, got, row0_ref, col0_ref, a_near, b_near, a_got, b_got,
+    sources_hbm, targets_hbm, rows_hbm, cols_hbm,
+    own, high, low,
+    sources, targets, rows, cols, a_ref, b_ref, row_ref, col_ref, own_high, own_low, sems,
 ):
-    a_ref, b_ref, row_ref, col_ref, own_high, own_low, sems = rest
     nodes = fetch(
         [
             (sources_hbm.at[1], sources),
@@ -286,12 +287,10 @@
         sems,
     )
     me = own_position(0)
-    tables = (a_ref, b_ref, row0_ref, col0_ref)
-    for index, lines in enumerate((packed, got)):
-        spread_sources(packed_source(lines), a_ref, b_ref)
+    for index, (lines, a0, b0) in enumerate(((packed, a_near, b_near), (got, a_got, b_got))):
 
         def mine(box, carry):
-            weigh(me, box, packed_target(lines), tables, own_high, own_low)
+            weigh(me, box, packed_target(lines), (a0, b0, row0_ref, col0_ref), own_high, own_low)
             start = pl.multiple_of(box * RHS, RHS)
             real = lines[pl.ds(start, RHS), :]
             imag = lines[pl.ds(start + BOXES * RHS, RHS), :]
@@ -451,36 +450,37 @@
             name="pack",
         )(far(current), *nodes)
         got = swapped(packed, "sy")
-        partial, row0, col0 = pl.pallas_call(
+        partial, row0, col0, a_near, b_near = pl.pallas_call(
             near_kernel,
             in_specs=[WHOLE] * 3,
-            out_specs=[WHOLE] * 3,
-            out_shape=[KEPT, SPREAD, SPREAD],
-            scratch_shapes=(COLUMNS, COLUMNS, PAIR, PAIR),
+            out_specs=[WHOLE] * 5,
+            out_shape=[KEPT, SPREAD, SPREAD, COLUMNS, COLUMNS],
+            scratch_shapes=(PAIR, PAIR),
             compiler_params=PARAMS,
             cost_estimate=cost(20_000_000),
             name="near",
         )(packed, rows, cols)
-        sent = pl.pallas_call(
+        sent, a_got, b_got = pl.pallas_call(
             partner_kernel,
             in_specs=[WHOLE] * 4,
-            out_specs=WHOLE,
-            out_shape=KEPT,
-            scratch_shapes=(COLUMNS, COLUMNS, PAIR, PAIR),
+            out_specs=[WHOLE] * 3,
+            out_shape=[KEPT, COLUMNS, COLUMNS],
+            scratch_shapes=(PAIR, PAIR),
             compiler_params=PARAMS,
             name="partner",
         )(got, row0, col0, partial)
-        made = pl.pallas_call(
+        own, high, low = pl.pallas_call(
             second_kernel,
-            in_specs=[WHOLE] * 4 + [ANY] * 4,
+            in_specs=[WHOLE] * 8 + [ANY] * 4,
             out_specs=[WHOLE] * 3,
             out_shape=[KEPT, MADE, MADE],
             scratch_shapes=node_buffers(None)
-            + (COLUMNS, COLUMNS, SPREAD, SPREAD, ONE, ONE, pltpu.SemaphoreType.DMA((4,))),
+            + TABLES
+            + (ONE, ONE, pltpu.SemaphoreType.DMA((4,))),
             compiler_params=PARAMS,
             cost_estimate=cost(60_000_000),
             name="second",
-        )(packed, got, row0, col0, *nodes)
+        )(packed, got, row0, col0, a_near, b_near, a_got, b_got, *nodes)
         pieces = swapped(sent, "sx")
         sent, current = pl.pallas_call(
             middle_kernel,
@@ -490,7 +490,7 @@
             scratch_shapes=(LEFT, STAGE, pltpu.SemaphoreType.DMA((FOREIGN,))),
             compiler_params=PARAMS,
             name="middle",
-        )(pieces, *made)
+        )(pieces, own, high, low)
         made = pl.pallas_call(
             between_kernel,
             in_specs=[WHOLE] + [ANY] * 4,

time: 41.9 us -> 41.1 us (0.981)
  Pallas kernels: 14.8 us -> 14.1 us
    pallas_call x3, Pallas kernels: 6.26 us -> 5.53 us  [the longest x1 3.82 us: local(): pl.pallas_call(second_kernel, in_specs=[WHOLE] * 8 + [ANY] * 4, out_specs...]
  transfers between devices with their start and end apart: 3 -> 3, of which waited for: 2 -> 2; matrix products, arithmetic and copies ran while one was open for 0% -> 0% of each run, Pallas kernels for 25% -> 24%
where the time goes in v4:
time: 41.1 us; the launch traced here: 40.7 us
  blocking collectives  15 us (36%)
  Pallas kernels  14.1 us (34%)
  starting transfers between devices  10.5 us (26%)
  waiting for transfers between devices  1.11 us (3%)
    all_to_all x1, blocking collectives, exchange(): lax.all_to_all(sent, ('sx', 'sy'), 0, 0, axis_index_groups=groups[level],...  15 us
    ppermute x2, starting transfers between devices, swapped(): return lax.ppermute(block, axis, [(i, i ^ 1) for i in range(count)])  6.85 us
    pallas_call x1, Pallas kernels, local(): pl.pallas_call(between_kernel, in_specs=[WHOLE] + [ANY] * 4, out_specs=[W...  5.1 us
    pallas_call x1, Pallas kernels, local(): pl.pallas_call(second_kernel, in_specs=[WHOLE] * 8 + [ANY] * 4, out_specs...  3.82 us
    all_to_all x1, starting transfers between devices, exchange(): lax.all_to_all(sent, ('sx', 'sy'), 0, 0, axis_index_groups=groups[level],...  3.68 us
    pallas_call x1, Pallas kernels, local(): pl.pallas_call(middle_kernel, in_specs=[WHOLE] * 4, out_specs=[ANY, WHOLE...  1.3 us
    pallas_call x1, Pallas kernels, local(): pl.pallas_call(pack_kernel, in_specs=[ANY] * 5, out_specs=[WHOLE] * 3, ou...  0.9 us
    pallas_call x1, Pallas kernels, local(): pl.pallas_call(near_kernel, in_specs=[WHOLE] * 3, out_specs=[WHOLE] * 5,...  0.87 us
  transfers between devices with their start and end apart: 3, of which 2 were waited for; matrix products, arithmetic and copies ran while one was open for 0% of the time, Pallas kernels for 24%

profile of v4, /device:TPU:16, one launch (start us, length us, event | category | flops | bytes accessed | tf_op | source)
XLA Modules:
  0.0 40.7 jit_solution(1809607517167174541)
XLA Ops:
  0.0 0.9 %pack.1 = (f32[88,256]{1,0:T(8,128)S(1)}, f32[2,16,16]{2,1,0:T(8,128)S(1)}, f32[2,16,16]{2,1,0:T(8,128)S(1)}) custom-call(f32[2,2,16,256]{3,2,1,0:T(8,128)} %bitcast.4, f32[3,2,2,1,256]{4,3,2,1,0:T(1,128)} %sources_hbm.5, f32[3,2,2,2,2,1,256]{6,5,4,3,2,1,0:T(1,128)} %targets_hbm.5, f32[3,2,16,16]{3,2,1,0:T(8,128)} %rows_hbm.5, f32[3,2,16,16]{3,2,1,0:T(8,128)} %cols_hbm.5), custom_call_target="tpu_custom_call" | custom-call | tf_op jit(solution)/shard_map/pack/pallas_call | solution.py:443
  0.9 1.9 %collective-permute-start = (f32[88,256]{1,0:T(8,128)S(1)}, f32[88,256]{1,0:T(8,128)S(1)}, u32[]{:S(2)}, u32[]{:S(2)}) collective-permute-start(f32[88,256]{1,0:T(8,128)S(1)} %get-tuple-element.26.packed), channel_id=1, source_target_pairs={{0,1},{1,0},{2,3},{3,2},{4,5},{5,4},{6,7},{7,6},{8,9},{9,8},{10,11... | collective-permute-start | bytes 270344 | tf_op jit(solution)/shard_map/ppermute | solution.py:51
  2.8 0.9 %near.1 = (f32[2,2,16,256]{3,2,1,0:T(8,128)S(1)}, f32[2,16,256]{2,1,0:T(8,128)S(1)}, f32[2,16,256]{2,1,0:T(8,128)S(1)}, f32[2,256,128]{2,1,0:T(8,128)S(1)}, f32[2,256,128]{2,1,0:T(8,128)S(1)}) custom-call(f32[88,256]{1,0:T(8,128)S(1)} %get-tuple-element.26.packed, f32[2,16,16]{2,1,0:T(8,128)S(1)} %get-tuple-element.27.rows, ...), custom_call_target="tpu_custom_call" | custom-call | flops 20000000 | bytes 100000 | tf_op jit(solution)/shard_map/near/pallas_call | solution.py:453
  3.7 0.4 collective-permute-done.packed.got
  4.1 0.8 %partner.1 = (f32[2,2,16,256]{3,2,1,0:T(8,128)S(1)}, f32[2,256,128]{2,1,0:T(8,128)S(1)}, f32[2,256,128]{2,1,0:T(8,128)S(1)}) custom-call(f32[88,256]{1,0:T(8,128)S(1)} %collective-permute-done.packed.got, f32[2,16,256]{2,1,0:T(8,128)S(1)} %get-tuple-element.29.row_ref.row0_ref, f32[2,16,256]{2,1,0:T(8,128)S(1)} %get-tuple-element.30.col_ref.col0_ref, ...), custom_call_target="tpu_custom_call" | custom-call | tf_op jit(solution)/shard_map/partner/pallas_call | solution.py:463
  5.0 4.9 %collective-permute-start.1 = (f32[2,2,16,256]{3,2,1,0:T(8,128)S(1)}, f32[2,2,16,256]{3,2,1,0:T(8,128)S(1)}, u32[]{:S(2)}, u32[]{:S(2)}) collective-permute-start(f32[2,2,16,256]{3,2,1,0:T(8,128)S(1)} %get-tuple-element.32), channel_id=1, source_target_pairs={{0,32},{32,0},{64,96},{96,64},{128,160},{160,128},{192,224},{224,1... | collective-permute-start | bytes 196616 | tf_op jit(solution)/shard_map/ppermute | solution.py:51
  9.9 3.8 %second.1 = (f32[2,2,16,256]{3,2,1,0:T(8,128)S(1)}, bf16[6,512,256]{2,1,0:T(8,128)(2,1)S(1)}, bf16[6,512,256]{2,1,0:T(8,128)(2,1)S(1)}) custom-call(f32[88,256]{1,0:T(8,128)S(1)} %get-tuple-element.26.packed, f32[88,256]{1,0:T(8,128)S(1)} %collective-permute-done.packed.got, f32[2,16,256]{2,1,0:T(8,128)S(1)} %get-tuple-element.29.row_ref.row0_ref, ...), custom_call_target="tpu_custom_call" | custom-call | flops 60000000 | bytes 100000 | tf_op jit(solution)/shard_map/second/pallas_call | solution.py:472
  13.7 0.0 collective-permute-done.1.piece
  13.7 1.3 %middle.1 = (f32[4,2,2,16,256]{4,3,2,1,0:T(8,128)}, f32[2,2,16,256]{3,2,1,0:T(8,128)S(1)}) custom-call(f32[2,2,16,256]{3,2,1,0:T(8,128)S(1)} %collective-permute-done.1.piece, f32[2,2,16,256]{3,2,1,0:T(8,128)S(1)} %get-tuple-element.37.own, bf16[6,512,256]{2,1,0:T(8,128)(2,1)S(1)} %get-tuple-element.38.high, bf16[6,512,256]{2,1,0:T(8,128)(2,1)S(1)} %get-tuple-element.39.low), custom_call_target="tpu_custom_call" | custom-call | tf_op jit(solution)/shard_map/middle/pallas_call | solution.py:485
  15.0 3.7 %all-to-all-start = ((f32[4,2,2,16,256]{4,3,2,1,0:T(8,128)}), f32[4,2,2,16,256]{4,3,2,1,0:T(8,128)S(1)}, u32[]{:S(2)}, u32[]{:S(2)}) async-start(f32[4,2,2,16,256]{4,3,2,1,0:T(8,128)} %get-tuple-element.40), calls=%async_computation | async-start | bytes 524288 | tf_op jit(solution)/shard_map/all_to_all | solution.py:431
  18.7 5.1 %between.1 = (f32[2,2,16,256]{3,2,1,0:T(8,128)S(1)}, bf16[8,512,256]{2,1,0:T(8,128)(2,1)S(1)}, f8e4m3fn[8,512,256]{2,1,0:T(32,128)(4,1)S(1)}, f32[2,128]{1,0:T(2,128)S(1)}, f32[2,128]{1,0:T(2,128)S(1)}) custom-call(f32[2,2,16,256]{3,2,1,0:T(8,128)S(1)} %get-tuple-element.41.values, f32[3,2,2,1,256]{4,3,2,1,0:T(1,128)} %sources_hbm.5, ...), custom_call_target="tpu_custom_call" | custom-call | flops 60000000 | bytes 100000 | tf_op jit(solution)/shard_map/between/pallas_call | solution.py:494
  23.8 0.7 %all-to-all-done.pieces = f32[4,2,2,16,256]{4,3,2,1,0:T(8,128)S(1)} async-done(((f32[4,2,2,16,256]{4,3,2,1,0:T(8,128)}), f32[4,2,2,16,256]{4,3,2,1,0:T(8,128)S(1)}, u32[]{:S(2)}, u32[]{:S(2)}) %all-to-all-start) | async-done | bytes 262176 | tf_op jit(solution)/shard_map/all_to_all | solution.py:431
  24.5 0.6 %late.1 = f32[4,2,2,16,256]{4,3,2,1,0:T(8,128)S(1)} custom-call(f32[4,2,2,16,256]{4,3,2,1,0:T(8,128)S(1)} %all-to-all-done.pieces, f32[2,2,16,256]{3,2,1,0:T(8,128)S(1)} %get-tuple-element.42.own, bf16[8,512,256]{2,1,0:T(8,128)(2,1)S(1)} %get-tuple-element.43.high, f8e4m3fn[8,512,256]{2,1,0:T(32,128)(4,1)S(1)} %get-tuple-element.44.low, ...), custom_call_target="tpu_custom_call" | custom-call | tf_op jit(solution)/shard_map/late/pallas_call | solution.py:513
  25.1 15.0 %all_to_all.10.pieces = f32[4,2,2,16,256]{4,3,2,1,0:T(8,128)S(1)} all-to-all(f32[4,2,2,16,256]{4,3,2,1,0:T(8,128)S(1)} %late.1), channel_id=1, replica_groups={{0,4,128,132},{1,5,129,133},{2,6,130,134},{3,7,131,135},{8,12,136,140},..., dimensions={0} | all-to-all | bytes 524288 | tf_op jit(solution)/shard_map/all_to_all | solution.py:431
  40.1 0.6 %final.1 = f32[2,2,16,256]{3,2,1,0:T(8,128)} custom-call(f32[4,2,2,16,256]{4,3,2,1,0:T(8,128)S(1)} %all_to_all.10.pieces), custom_call_target="tpu_custom_call" | custom-call | tf_op jit(solution)/shard_map/final/pallas_call | solution.py:522
Async XLA Ops:
  0.9 3.2 %collective-permute-start = (f32[88,256]{1,0:T(8,128)S(1)}, f32[88,256]{1,0:T(8,128)S(1)}, u32[]{:S(2)}, u32[]{:S(2)}) collective-permute-start(f32[88,256]{1,0:T(8,128)S(1)} %get-tuple-element.26.packed), channel_id=1, source_target_pairs={{0,1},{1,0},{2,3},{3,2},{4,5},{5,4},{6,7},{7,6},{8,9},{9,8},{10,11... | collective-permute-start | bytes 270344 | tf_op jit(solution)/shard_map/ppermute | solution.py:51
  5.0 8.8 %collective-permute-start.1 = (f32[2,2,16,256]{3,2,1,0:T(8,128)S(1)}, f32[2,2,16,256]{3,2,1,0:T(8,128)S(1)}, u32[]{:S(2)}, u32[]{:S(2)}) collective-permute-start(f32[2,2,16,256]{3,2,1,0:T(8,128)S(1)} %get-tuple-element.32), channel_id=1, source_target_pairs={{0,32},{32,0},{64,96},{96,64},{128,160},{160,128},{192,224},{224,1... | collective-permute-start | bytes 196616 | tf_op jit(solution)/shard_map/ppermute | solution.py:51
  15.0 9.5 %all-to-all-start = ((f32[4,2,2,16,256]{4,3,2,1,0:T(8,128)}), f32[4,2,2,16,256]{4,3,2,1,0:T(8,128)S(1)}, u32[]{:S(2)}, u32[]{:S(2)}) async-start(f32[4,2,2,16,256]{4,3,2,1,0:T(8,128)} %get-tuple-element.40), calls=%async_computation | async-start | bytes 524288 | tf_op jit(solution)/shard_map/all_to_all | solution.py:431

commit v5 on v4

--- a/solution.py
+++ b/solution.py
@@ -257,18 +257,15 @@
 def make_weights(level, first, targets, tables, high, low):
     there = own_position(level)
 
-    def make(item, carry):
-        weigh(
-            there ^ (item // 2 + first),
-            item % 2,
-            line_of(targets),
-            tables,
-            high.at[item],
-            low.at[item],
-        )
+    def make(step, carry):
+        for box in range(BOXES):
+            item = BOXES * step + box
+            weigh(
+                there ^ (step + first), box, line_of(targets), tables, high.at[item], low.at[item]
+            )
         return carry
 
-    lax.fori_loop(0, (4 - first) * BOXES, make, 0)
+    lax.fori_loop(0, 4 - first, make, 0)
 
 
 def second_kernel(
@@ -287,24 +284,14 @@
         sems,
     )
     me = own_position(0)
-    for index, (lines, a0, b0) in enumerate(((packed, a_near, b_near), (got, a_got, b_got))):
-
-        def mine(box, carry):
-            weigh(me, box, packed_target(lines), (a0, b0, row0_ref, col0_ref), own_high, own_low)
-            start = pl.multiple_of(box * RHS, RHS)
-            real = lines[pl.ds(start, RHS), :]
-            imag = lines[pl.ds(start + BOXES * RHS, RHS), :]
-            left = stacked(jnp.concatenate([real, imag], axis=0))
-            total = product(left, own_high[...], own_low[...])
-            if index:
-                own[0, box] += total[:RHS]
-                own[1, box] += total[RHS:]
-            else:
-                own[0, box] = total[:RHS]
-                own[1, box] = total[RHS:]
-            return carry
-
-        lax.fori_loop(0, BOXES, mine, 0)
+    halves = [
+        pair_of_boxes(lines, me, (a0, b0, row0_ref, col0_ref), own_high, own_low)
+        for lines, a0, b0 in ((packed, a_near, b_near), (got, a_got, b_got))
+    ]
+    for box in range(BOXES):
+        total = halves[0][box] + halves[1][box]
+        own[0, box] = total[:RHS]
+        own[1, box] = total[RHS:]
     for copy in nodes:
         copy.wait()
     tables = (a_ref, b_ref, row_ref, col_ref)
@@ -333,14 +320,12 @@
     prepare(sources.at[0], rows.at[0], cols.at[0], tables)
     me = own_position(1)
 
-    def mine(box, carry):
-        weigh(me, box, line_of(targets.at[0]), tables, own_high, own_low)
-        total = product(left[box], own_high[...], own_low[...])
+    for box in range(BOXES):
+        weigh(me, box, line_of(targets.at[0]), tables, own_high.at[box], own_low.at[box])
+    for box in range(BOXES):
+        total = product(left[box], own_high[box], own_low[box])
         own[0, box] = total[:RHS]
         own[1, box] = total[RHS:]
-        return carry
-
-    lax.fori_loop(0, BOXES, mine, 0)
     normalize(rows.at[1], row_normal, row_size)
     normalize(cols.at[1], col_normal, col_size)
     prepare(sources.at[1], row_normal, col_normal, tables)
@@ -410,7 +395,6 @@
 KEPT = pltpu.VMEM(FIELD, jnp.float32)
 SPREAD = pltpu.VMEM((2, CHEB, NODES), jnp.float32)
 SMALL = pltpu.VMEM((2, CHEB, CHEB), jnp.float32)
-ONE = pltpu.VMEM((2 * NODES, NODES), jnp.bfloat16)
 PAIR = pltpu.VMEM((BOXES, 2 * NODES, NODES), jnp.bfloat16)
 COLUMNS = pltpu.VMEM((BOXES, NODES, 128), jnp.float32)
 MADE = pltpu.VMEM((ITEMS, 2 * NODES, NODES), jnp.bfloat16)
@@ -476,7 +460,7 @@
             out_shape=[KEPT, MADE, MADE],
             scratch_shapes=node_buffers(None)
             + TABLES
-            + (ONE, ONE, pltpu.SemaphoreType.DMA((4,))),
+            + (PAIR, PAIR, pltpu.SemaphoreType.DMA((4,))),
             compiler_params=PARAMS,
             cost_estimate=cost(60_000_000),
             name="second",
@@ -504,7 +488,7 @@
             ],
             scratch_shapes=node_buffers(2)
             + TABLES
-            + (ONE, ONE, LEFT, SMALL, SMALL, pltpu.SemaphoreType.DMA((4,))),
+            + (PAIR, PAIR, LEFT, SMALL, SMALL, pltpu.SemaphoreType.DMA((4,))),
             compiler_params=PARAMS,
             cost_estimate=cost(60_000_000),
             name="between",

time: 41.1 us -> 40.8 us (level)
  Pallas kernels: 14.1 us -> 13.4 us
  waiting for transfers between devices: 1.11 us -> 1.8 us
    all_to_all x1, waiting for transfers between devices: 0.73 us -> 1.41 us  [exchange(): lax.all_to_all(sent, ('sx', 'sy'), 0, 0, axis_index_groups=groups[level],...]
    pallas_call x1, Pallas kernels: 5.1 us -> 4.41 us  [local(): pl.pallas_call(between_kernel, in_specs=[WHOLE] + [ANY] * 4, out_specs=[W...]
  transfers between devices with their start and end apart: 3 -> 3, of which waited for: 2 -> 2; matrix products, arithmetic and copies ran while one was open for 0% -> 0% of each run, Pallas kernels for 24% -> 22%
where the time goes in v5:
time: 40.8 us; the launch traced here: 40.4 us
  blocking collectives  14.6 us (36%)
  Pallas kernels  13.4 us (33%)
  starting transfers between devices  10.5 us (26%)
  waiting for transfers between devices  1.8 us (4%)
    all_to_all x1, blocking collectives, exchange(): lax.all_to_all(sent, ('sx', 'sy'), 0, 0, axis_index_groups=groups[level],...  14.6 us
    ppermute x2, starting transfers between devices, swapped(): return lax.ppermute(block, axis, [(i, i ^ 1) for i in range(count)])  6.85 us
    pallas_call x1, Pallas kernels, local(): pl.pallas_call(between_kernel, in_specs=[WHOLE] + [ANY] * 4, out_specs=[W...  4.41 us
    pallas_call x1, Pallas kernels, local(): pl.pallas_call(second_kernel, in_specs=[WHOLE] * 8 + [ANY] * 4, out_specs...  3.8 us
    all_to_all x1, starting transfers between devices, exchange(): lax.all_to_all(sent, ('sx', 'sy'), 0, 0, axis_index_groups=groups[level],...  3.68 us
    all_to_all x1, waiting for transfers between devices, exchange(): lax.all_to_all(sent, ('sx', 'sy'), 0, 0, axis_index_groups=groups[level],...  1.41 us
    pallas_call x1, Pallas kernels, local(): pl.pallas_call(middle_kernel, in_specs=[WHOLE] * 4, out_specs=[ANY, WHOLE...  1.3 us
    pallas_call x1, Pallas kernels, local(): pl.pallas_call(pack_kernel, in_specs=[ANY] * 5, out_specs=[WHOLE] * 3, ou...  0.9 us
  transfers between devices with their start and end apart: 3, of which 2 were waited for; matrix products, arithmetic and copies ran while one was open for 0% of the time, Pallas kernels for 22%

profile of v5, /device:TPU:16, one launch (start us, length us, event | category | flops | bytes accessed | tf_op | source)
XLA Modules:
  0.0 40.4 jit_solution(97159630762363246)
XLA Ops:
  0.0 0.9 %pack.1 = (f32[88,256]{1,0:T(8,128)S(1)}, f32[2,16,16]{2,1,0:T(8,128)S(1)}, f32[2,16,16]{2,1,0:T(8,128)S(1)}) custom-call(f32[2,2,16,256]{3,2,1,0:T(8,128)} %bitcast.4, f32[3,2,2,1,256]{4,3,2,1,0:T(1,128)} %sources_hbm.5, f32[3,2,2,2,2,1,256]{6,5,4,3,2,1,0:T(1,128)} %targets_hbm.5, f32[3,2,16,16]{3,2,1,0:T(8,128)} %rows_hbm.5, f32[3,2,16,16]{3,2,1,0:T(8,128)} %cols_hbm.5), custom_call_target="tpu_custom_call" | custom-call | tf_op jit(solution)/shard_map/pack/pallas_call | solution.py:427
  0.9 1.9 %collective-permute-start = (f32[88,256]{1,0:T(8,128)S(1)}, f32[88,256]{1,0:T(8,128)S(1)}, u32[]{:S(2)}, u32[]{:S(2)}) collective-permute-start(f32[88,256]{1,0:T(8,128)S(1)} %get-tuple-element.26.packed), channel_id=1, source_target_pairs={{0,1},{1,0},{2,3},{3,2},{4,5},{5,4},{6,7},{7,6},{8,9},{9,8},{10,11... | collective-permute-start | bytes 270344 | tf_op jit(solution)/shard_map/ppermute | solution.py:51
  2.8 0.9 %near.1 = (f32[2,2,16,256]{3,2,1,0:T(8,128)S(1)}, f32[2,16,256]{2,1,0:T(8,128)S(1)}, f32[2,16,256]{2,1,0:T(8,128)S(1)}, f32[2,256,128]{2,1,0:T(8,128)S(1)}, f32[2,256,128]{2,1,0:T(8,128)S(1)}) custom-call(f32[88,256]{1,0:T(8,128)S(1)} %get-tuple-element.26.packed, f32[2,16,16]{2,1,0:T(8,128)S(1)} %get-tuple-element.27.rows, ...), custom_call_target="tpu_custom_call" | custom-call | flops 20000000 | bytes 100000 | tf_op jit(solution)/shard_map/near/pallas_call | solution.py:437
  3.7 0.4 collective-permute-done.packed.got
  4.1 0.8 %partner.1 = (f32[2,2,16,256]{3,2,1,0:T(8,128)S(1)}, f32[2,256,128]{2,1,0:T(8,128)S(1)}, f32[2,256,128]{2,1,0:T(8,128)S(1)}) custom-call(f32[88,256]{1,0:T(8,128)S(1)} %collective-permute-done.packed.got, f32[2,16,256]{2,1,0:T(8,128)S(1)} %get-tuple-element.29.row_ref.row0_ref, f32[2,16,256]{2,1,0:T(8,128)S(1)} %get-tuple-element.30.col_ref.col0_ref, ...), custom_call_target="tpu_custom_call" | custom-call | tf_op jit(solution)/shard_map/partner/pallas_call | solution.py:447
  5.0 4.9 %collective-permute-start.1 = (f32[2,2,16,256]{3,2,1,0:T(8,128)S(1)}, f32[2,2,16,256]{3,2,1,0:T(8,128)S(1)}, u32[]{:S(2)}, u32[]{:S(2)}) collective-permute-start(f32[2,2,16,256]{3,2,1,0:T(8,128)S(1)} %get-tuple-element.32), channel_id=1, source_target_pairs={{0,32},{32,0},{64,96},{96,64},{128,160},{160,128},{192,224},{224,1... | collective-permute-start | bytes 196616 | tf_op jit(solution)/shard_map/ppermute | solution.py:51
  9.9 3.8 %second.1 = (f32[2,2,16,256]{3,2,1,0:T(8,128)S(1)}, bf16[6,512,256]{2,1,0:T(8,128)(2,1)S(1)}, bf16[6,512,256]{2,1,0:T(8,128)(2,1)S(1)}) custom-call(f32[88,256]{1,0:T(8,128)S(1)} %get-tuple-element.26.packed, f32[88,256]{1,0:T(8,128)S(1)} %collective-permute-done.packed.got, f32[2,16,256]{2,1,0:T(8,128)S(1)} %get-tuple-element.29.row_ref.row0_ref, ...), custom_call_target="tpu_custom_call" | custom-call | flops 60000000 | bytes 100000 | tf_op jit(solution)/shard_map/second/pallas_call | solution.py:456
  13.7 0.0 collective-permute-done.1.piece
  13.7 1.3 %middle.1 = (f32[4,2,2,16,256]{4,3,2,1,0:T(8,128)}, f32[2,2,16,256]{3,2,1,0:T(8,128)S(1)}) custom-call(f32[2,2,16,256]{3,2,1,0:T(8,128)S(1)} %collective-permute-done.1.piece, f32[2,2,16,256]{3,2,1,0:T(8,128)S(1)} %get-tuple-element.37.own, bf16[6,512,256]{2,1,0:T(8,128)(2,1)S(1)} %get-tuple-element.38.high, bf16[6,512,256]{2,1,0:T(8,128)(2,1)S(1)} %get-tuple-element.39.low), custom_call_target="tpu_custom_call" | custom-call | tf_op jit(solution)/shard_map/middle/pallas_call | solution.py:469
  15.0 3.7 %all-to-all-start = ((f32[4,2,2,16,256]{4,3,2,1,0:T(8,128)}), f32[4,2,2,16,256]{4,3,2,1,0:T(8,128)S(1)}, u32[]{:S(2)}, u32[]{:S(2)}) async-start(f32[4,2,2,16,256]{4,3,2,1,0:T(8,128)} %get-tuple-element.40), calls=%async_computation | async-start | bytes 524288 | tf_op jit(solution)/shard_map/all_to_all | solution.py:415
  18.7 4.4 %between.1 = (f32[2,2,16,256]{3,2,1,0:T(8,128)S(1)}, bf16[8,512,256]{2,1,0:T(8,128)(2,1)S(1)}, f8e4m3fn[8,512,256]{2,1,0:T(32,128)(4,1)S(1)}, f32[2,128]{1,0:T(2,128)S(1)}, f32[2,128]{1,0:T(2,128)S(1)}) custom-call(f32[2,2,16,256]{3,2,1,0:T(8,128)S(1)} %get-tuple-element.41.values, f32[3,2,2,1,256]{4,3,2,1,0:T(1,128)} %sources_hbm.5, ...), custom_call_target="tpu_custom_call" | custom-call | flops 60000000 | bytes 100000 | tf_op jit(solution)/shard_map/between/pallas_call | solution.py:478
  23.1 1.4 %all-to-all-done.pieces = f32[4,2,2,16,256]{4,3,2,1,0:T(8,128)S(1)} async-done(((f32[4,2,2,16,256]{4,3,2,1,0:T(8,128)}), f32[4,2,2,16,256]{4,3,2,1,0:T(8,128)S(1)}, u32[]{:S(2)}, u32[]{:S(2)}) %all-to-all-start) | async-done | bytes 262176 | tf_op jit(solution)/shard_map/all_to_all | solution.py:415
  24.5 0.6 %late.1 = f32[4,2,2,16,256]{4,3,2,1,0:T(8,128)S(1)} custom-call(f32[4,2,2,16,256]{4,3,2,1,0:T(8,128)S(1)} %all-to-all-done.pieces, f32[2,2,16,256]{3,2,1,0:T(8,128)S(1)} %get-tuple-element.42.own, bf16[8,512,256]{2,1,0:T(8,128)(2,1)S(1)} %get-tuple-element.43.high, f8e4m3fn[8,512,256]{2,1,0:T(32,128)(4,1)S(1)} %get-tuple-element.44.low, ...), custom_call_target="tpu_custom_call" | custom-call | tf_op jit(solution)/shard_map/late/pallas_call | solution.py:497
  25.1 14.6 %all_to_all.10.pieces = f32[4,2,2,16,256]{4,3,2,1,0:T(8,128)S(1)} all-to-all(f32[4,2,2,16,256]{4,3,2,1,0:T(8,128)S(1)} %late.1), channel_id=1, replica_groups={{0,4,128,132},{1,5,129,133},{2,6,130,134},{3,7,131,135},{8,12,136,140},..., dimensions={0} | all-to-all | bytes 524288 | tf_op jit(solution)/shard_map/all_to_all | solution.py:415
  39.7 0.6 %final.1 = f32[2,2,16,256]{3,2,1,0:T(8,128)} custom-call(f32[4,2,2,16,256]{4,3,2,1,0:T(8,128)S(1)} %all_to_all.10.pieces), custom_call_target="tpu_custom_call" | custom-call | tf_op jit(solution)/shard_map/final/pallas_call | solution.py:506
Async XLA Ops:
  0.9 3.2 %collective-permute-start = (f32[88,256]{1,0:T(8,128)S(1)}, f32[88,256]{1,0:T(8,128)S(1)}, u32[]{:S(2)}, u32[]{:S(2)}) collective-permute-start(f32[88,256]{1,0:T(8,128)S(1)} %get-tuple-element.26.packed), channel_id=1, source_target_pairs={{0,1},{1,0},{2,3},{3,2},{4,5},{5,4},{6,7},{7,6},{8,9},{9,8},{10,11... | collective-permute-start | bytes 270344 | tf_op jit(solution)/shard_map/ppermute | solution.py:51
  5.0 8.8 %collective-permute-start.1 = (f32[2,2,16,256]{3,2,1,0:T(8,128)S(1)}, f32[2,2,16,256]{3,2,1,0:T(8,128)S(1)}, u32[]{:S(2)}, u32[]{:S(2)}) collective-permute-start(f32[2,2,16,256]{3,2,1,0:T(8,128)S(1)} %get-tuple-element.32), channel_id=1, source_target_pairs={{0,32},{32,0},{64,96},{96,64},{128,160},{160,128},{192,224},{224,1... | collective-permute-start | bytes 196616 | tf_op jit(solution)/shard_map/ppermute | solution.py:51
  15.0 9.5 %all-to-all-start = ((f32[4,2,2,16,256]{4,3,2,1,0:T(8,128)}), f32[4,2,2,16,256]{4,3,2,1,0:T(8,128)S(1)}, u32[]{:S(2)}, u32[]{:S(2)}) async-start(f32[4,2,2,16,256]{4,3,2,1,0:T(8,128)} %get-tuple-element.40), calls=%async_computation | async-start | bytes 524288 | tf_op jit(solution)/shard_map/all_to_all | solution.py:415

commit v6 on v5

--- a/solution.py
+++ b/solution.py
@@ -284,14 +284,24 @@
         sems,
     )
     me = own_position(0)
-    halves = [
-        pair_of_boxes(lines, me, (a0, b0, row0_ref, col0_ref), own_high, own_low)
-        for lines, a0, b0 in ((packed, a_near, b_near), (got, a_got, b_got))
-    ]
-    for box in range(BOXES):
-        total = halves[0][box] + halves[1][box]
+    places = ((packed, a_near, b_near), (got, a_got, b_got))
+
+    def mine(box, carry):
+        for index, (lines, a0, b0) in enumerate(places):
+            tables = (a0, b0, row0_ref, col0_ref)
+            weigh(me, box, packed_target(lines), tables, own_high.at[index], own_low.at[index])
+        total = 0.0
+        for index, (lines, a0, b0) in enumerate(places):
+            start = pl.multiple_of(box * RHS, RHS)
+            real = lines[pl.ds(start, RHS), :]
+            imag = lines[pl.ds(start + BOXES * RHS, RHS), :]
+            left = stacked(jnp.concatenate([real, imag], axis=0))
+            total = total + product(left, own_high[index], own_low[index])
         own[0, box] = total[:RHS]
         own[1, box] = total[RHS:]
+        return carry
+
+    lax.fori_loop(0, BOXES, mine, 0)
     for copy in nodes:
         copy.wait()
     tables = (a_ref, b_ref, row_ref, col_ref)

time: 40.8 us -> 40.4 us (level)
  no operation moved by 1% of the time
where the time goes in v6:
time: 40.4 us; the launch traced here: 40 us
  blocking collectives  14.6 us (36%)
  Pallas kernels  13 us (32%)
  starting transfers between devices  10.7 us (26%)
  waiting for transfers between devices  1.6 us (4%)
    all_to_all x1, blocking collectives, exchange(): lax.all_to_all(sent, ('sx', 'sy'), 0, 0, axis_index_groups=groups[level],...  14.6 us
    ppermute x2, starting transfers between devices, swapped(): return lax.ppermute(block, axis, [(i, i ^ 1) for i in range(count)])  6.85 us
    pallas_call x1, Pallas kernels, local(): pl.pallas_call(between_kernel, in_specs=[WHOLE] + [ANY] * 4, out_specs=[W...  4.41 us
    all_to_all x1, starting transfers between devices, exchange(): lax.all_to_all(sent, ('sx', 'sy'), 0, 0, axis_index_groups=groups[level],...  3.88 us
    pallas_call x1, Pallas kernels, local(): pl.pallas_call(second_kernel, in_specs=[WHOLE] * 8 + [ANY] * 4, out_specs...  3.4 us
    pallas_call x1, Pallas kernels, local(): pl.pallas_call(middle_kernel, in_specs=[WHOLE] * 4, out_specs=[ANY, WHOLE...  1.3 us
    all_to_all x1, waiting for transfers between devices, exchange(): lax.all_to_all(sent, ('sx', 'sy'), 0, 0, axis_index_groups=groups[level],...  1.21 us
    pallas_call x1, Pallas kernels, local(): pl.pallas_call(pack_kernel, in_specs=[ANY] * 5, out_specs=[WHOLE] * 3, ou...  0.9 us
  transfers between devices with their start and end apart: 3, of which 2 were waited for; matrix products, arithmetic and copies ran while one was open for 0% of the time, Pallas kernels for 22%

profile of v6, /device:TPU:16, one launch (start us, length us, event | category | flops | bytes accessed | tf_op | source)
XLA Modules:
  0.0 40.0 jit_solution(4949756095058428840)
XLA Ops:
  0.0 0.9 %pack.1 = (f32[88,256]{1,0:T(8,128)S(1)}, f32[2,16,16]{2,1,0:T(8,128)S(1)}, f32[2,16,16]{2,1,0:T(8,128)S(1)}) custom-call(f32[2,2,16,256]{3,2,1,0:T(8,128)} %bitcast.4, f32[3,2,2,1,256]{4,3,2,1,0:T(1,128)} %sources_hbm.5, f32[3,2,2,2,2,1,256]{6,5,4,3,2,1,0:T(1,128)} %targets_hbm.5, f32[3,2,16,16]{3,2,1,0:T(8,128)} %rows_hbm.5, f32[3,2,16,16]{3,2,1,0:T(8,128)} %cols_hbm.5), custom_call_target="tpu_custom_call" | custom-call | tf_op jit(solution)/shard_map/pack/pallas_call | solution.py:437
  0.9 1.9 %collective-permute-start = (f32[88,256]{1,0:T(8,128)S(1)}, f32[88,256]{1,0:T(8,128)S(1)}, u32[]{:S(2)}, u32[]{:S(2)}) collective-permute-start(f32[88,256]{1,0:T(8,128)S(1)} %get-tuple-element.26.packed), channel_id=1, source_target_pairs={{0,1},{1,0},{2,3},{3,2},{4,5},{5,4},{6,7},{7,6},{8,9},{9,8},{10,11... | collective-permute-start | bytes 270344 | tf_op jit(solution)/shard_map/ppermute | solution.py:51
  2.8 0.9 %near.1 = (f32[2,2,16,256]{3,2,1,0:T(8,128)S(1)}, f32[2,16,256]{2,1,0:T(8,128)S(1)}, f32[2,16,256]{2,1,0:T(8,128)S(1)}, f32[2,256,128]{2,1,0:T(8,128)S(1)}, f32[2,256,128]{2,1,0:T(8,128)S(1)}) custom-call(f32[88,256]{1,0:T(8,128)S(1)} %get-tuple-element.26.packed, f32[2,16,16]{2,1,0:T(8,128)S(1)} %get-tuple-element.27.rows, ...), custom_call_target="tpu_custom_call" | custom-call | flops 20000000 | bytes 100000 | tf_op jit(solution)/shard_map/near/pallas_call | solution.py:447
  3.7 0.4 collective-permute-done.packed.got
  4.1 0.8 %partner.1 = (f32[2,2,16,256]{3,2,1,0:T(8,128)S(1)}, f32[2,256,128]{2,1,0:T(8,128)S(1)}, f32[2,256,128]{2,1,0:T(8,128)S(1)}) custom-call(f32[88,256]{1,0:T(8,128)S(1)} %collective-permute-done.packed.got, f32[2,16,256]{2,1,0:T(8,128)S(1)} %get-tuple-element.29.row_ref.row0_ref, f32[2,16,256]{2,1,0:T(8,128)S(1)} %get-tuple-element.30.col_ref.col0_ref, ...), custom_call_target="tpu_custom_call" | custom-call | tf_op jit(solution)/shard_map/partner/pallas_call | solution.py:457
  5.0 4.9 %collective-permute-start.1 = (f32[2,2,16,256]{3,2,1,0:T(8,128)S(1)}, f32[2,2,16,256]{3,2,1,0:T(8,128)S(1)}, u32[]{:S(2)}, u32[]{:S(2)}) collective-permute-start(f32[2,2,16,256]{3,2,1,0:T(8,128)S(1)} %get-tuple-element.32), channel_id=1, source_target_pairs={{0,32},{32,0},{64,96},{96,64},{128,160},{160,128},{192,224},{224,1... | collective-permute-start | bytes 196616 | tf_op jit(solution)/shard_map/ppermute | solution.py:51
  9.9 3.4 %second.1 = (f32[2,2,16,256]{3,2,1,0:T(8,128)S(1)}, bf16[6,512,256]{2,1,0:T(8,128)(2,1)S(1)}, bf16[6,512,256]{2,1,0:T(8,128)(2,1)S(1)}) custom-call(f32[88,256]{1,0:T(8,128)S(1)} %get-tuple-element.26.packed, f32[88,256]{1,0:T(8,128)S(1)} %collective-permute-done.packed.got, f32[2,16,256]{2,1,0:T(8,128)S(1)} %get-tuple-element.29.row_ref.row0_ref, ...), custom_call_target="tpu_custom_call" | custom-call | flops 60000000 | bytes 100000 | tf_op jit(solution)/shard_map/second/pallas_call | solution.py:466
  13.3 0.0 collective-permute-done.1.piece
  13.3 1.3 %middle.1 = (f32[4,2,2,16,256]{4,3,2,1,0:T(8,128)}, f32[2,2,16,256]{3,2,1,0:T(8,128)S(1)}) custom-call(f32[2,2,16,256]{3,2,1,0:T(8,128)S(1)} %collective-permute-done.1.piece, f32[2,2,16,256]{3,2,1,0:T(8,128)S(1)} %get-tuple-element.37.own, bf16[6,512,256]{2,1,0:T(8,128)(2,1)S(1)} %get-tuple-element.38.high, bf16[6,512,256]{2,1,0:T(8,128)(2,1)S(1)} %get-tuple-element.39.low), custom_call_target="tpu_custom_call" | custom-call | tf_op jit(solution)/shard_map/middle/pallas_call | solution.py:479
  14.6 3.9 %all-to-all-start = ((f32[4,2,2,16,256]{4,3,2,1,0:T(8,128)}), f32[4,2,2,16,256]{4,3,2,1,0:T(8,128)S(1)}, u32[]{:S(2)}, u32[]{:S(2)}) async-start(f32[4,2,2,16,256]{4,3,2,1,0:T(8,128)} %get-tuple-element.40), calls=%async_computation | async-start | bytes 524288 | tf_op jit(solution)/shard_map/all_to_all | solution.py:425
  18.5 4.4 %between.1 = (f32[2,2,16,256]{3,2,1,0:T(8,128)S(1)}, bf16[8,512,256]{2,1,0:T(8,128)(2,1)S(1)}, f8e4m3fn[8,512,256]{2,1,0:T(32,128)(4,1)S(1)}, f32[2,128]{1,0:T(2,128)S(1)}, f32[2,128]{1,0:T(2,128)S(1)}) custom-call(f32[2,2,16,256]{3,2,1,0:T(8,128)S(1)} %get-tuple-element.41.values, f32[3,2,2,1,256]{4,3,2,1,0:T(1,128)} %sources_hbm.5, ...), custom_call_target="tpu_custom_call" | custom-call | flops 60000000 | bytes 100000 | tf_op jit(solution)/shard_map/between/pallas_call | solution.py:488
  22.9 1.2 %all-to-all-done.pieces = f32[4,2,2,16,256]{4,3,2,1,0:T(8,128)S(1)} async-done(((f32[4,2,2,16,256]{4,3,2,1,0:T(8,128)}), f32[4,2,2,16,256]{4,3,2,1,0:T(8,128)S(1)}, u32[]{:S(2)}, u32[]{:S(2)}) %all-to-all-start) | async-done | bytes 262176 | tf_op jit(solution)/shard_map/all_to_all | solution.py:425
  24.1 0.6 %late.1 = f32[4,2,2,16,256]{4,3,2,1,0:T(8,128)S(1)} custom-call(f32[4,2,2,16,256]{4,3,2,1,0:T(8,128)S(1)} %all-to-all-done.pieces, f32[2,2,16,256]{3,2,1,0:T(8,128)S(1)} %get-tuple-element.42.own, bf16[8,512,256]{2,1,0:T(8,128)(2,1)S(1)} %get-tuple-element.43.high, f8e4m3fn[8,512,256]{2,1,0:T(32,128)(4,1)S(1)} %get-tuple-element.44.low, ...), custom_call_target="tpu_custom_call" | custom-call | tf_op jit(solution)/shard_map/late/pallas_call | solution.py:507
  24.7 14.6 %all_to_all.10.pieces = f32[4,2,2,16,256]{4,3,2,1,0:T(8,128)S(1)} all-to-all(f32[4,2,2,16,256]{4,3,2,1,0:T(8,128)S(1)} %late.1), channel_id=1, replica_groups={{0,4,128,132},{1,5,129,133},{2,6,130,134},{3,7,131,135},{8,12,136,140},..., dimensions={0} | all-to-all | bytes 524288 | tf_op jit(solution)/shard_map/all_to_all | solution.py:425
  39.3 0.6 %final.1 = f32[2,2,16,256]{3,2,1,0:T(8,128)} custom-call(f32[4,2,2,16,256]{4,3,2,1,0:T(8,128)S(1)} %all_to_all.10.pieces), custom_call_target="tpu_custom_call" | custom-call | tf_op jit(solution)/shard_map/final/pallas_call | solution.py:516
Async XLA Ops:
  0.9 3.2 %collective-permute-start = (f32[88,256]{1,0:T(8,128)S(1)}, f32[88,256]{1,0:T(8,128)S(1)}, u32[]{:S(2)}, u32[]{:S(2)}) collective-permute-start(f32[88,256]{1,0:T(8,128)S(1)} %get-tuple-element.26.packed), channel_id=1, source_target_pairs={{0,1},{1,0},{2,3},{3,2},{4,5},{5,4},{6,7},{7,6},{8,9},{9,8},{10,11... | collective-permute-start | bytes 270344 | tf_op jit(solution)/shard_map/ppermute | solution.py:51
  5.0 8.3 %collective-permute-start.1 = (f32[2,2,16,256]{3,2,1,0:T(8,128)S(1)}, f32[2,2,16,256]{3,2,1,0:T(8,128)S(1)}, u32[]{:S(2)}, u32[]{:S(2)}) collective-permute-start(f32[2,2,16,256]{3,2,1,0:T(8,128)S(1)} %get-tuple-element.32), channel_id=1, source_target_pairs={{0,32},{32,0},{64,96},{96,64},{128,160},{160,128},{192,224},{224,1... | collective-permute-start | bytes 196616 | tf_op jit(solution)/shard_map/ppermute | solution.py:51
  14.6 9.5 %all-to-all-start = ((f32[4,2,2,16,256]{4,3,2,1,0:T(8,128)}), f32[4,2,2,16,256]{4,3,2,1,0:T(8,128)S(1)}, u32[]{:S(2)}, u32[]{:S(2)}) async-start(f32[4,2,2,16,256]{4,3,2,1,0:T(8,128)} %get-tuple-element.40), calls=%async_computation | async-start | bytes 524288 | tf_op jit(solution)/shard_map/all_to_all | solution.py:425

commit v7 on v6

--- a/solution.py
+++ b/solution.py
@@ -235,7 +235,20 @@
     ]
 
 
-def near_kernel(packed, rows, cols, partial, row_ref, col_ref, a_ref, b_ref, high, low):
+def near_kernel(
+    packed, rows, cols, sources_hbm, targets_hbm, rows_hbm, cols_hbm,
+    partial, row_ref, col_ref, a_ref, b_ref, a1_ref, b1_ref, row1_ref, col1_ref, targets1,
+    high, low, sources1, rows1, cols1, sems,
+):
+    nodes = fetch(
+        [
+            (sources_hbm.at[1], sources1),
+            (rows_hbm.at[1], rows1),
+            (cols_hbm.at[1], cols1),
+            (targets_hbm.at[1], targets1),
+        ],
+        sems,
+    )
     spread_matrices(rows, cols, row_ref, col_ref)
     spread_sources(packed_source(packed), a_ref, b_ref)
     tables = (a_ref, b_ref, row_ref, col_ref)
@@ -243,6 +256,9 @@
     for box in range(BOXES):
         partial[0, box] = both[box][:RHS]
         partial[1, box] = both[box][RHS:]
+    for copy in nodes:
+        copy.wait()
+    prepare(sources1, rows1, cols1, (a1_ref, b1_ref, row1_ref, col1_ref))
 
 
 def partner_kernel(packed, row_ref, col_ref, partial, sent, a_ref, b_ref, high, low):
@@ -270,19 +286,9 @@
 
 def second_kernel(
     packed, got, row0_ref, col0_ref, a_near, b_near, a_got, b_got,
-    sources_hbm, targets_hbm, rows_hbm, cols_hbm,
-    own, high, low,
-    sources, targets, rows, cols, a_ref, b_ref, row_ref, col_ref, own_high, own_low, sems,
+    a_ref, b_ref, row_ref, col_ref, targets,
+    own, high, low, own_high, own_low,
 ):
-    nodes = fetch(
-        [
-            (sources_hbm.at[1], sources),
-            (rows_hbm.at[1], rows),
-            (cols_hbm.at[1], cols),
-            (targets_hbm.at[1], targets),
-        ],
-        sems,
-    )
     me = own_position(0)
     places = ((packed, a_near, b_near), (got, a_got, b_got))
 
@@ -302,11 +308,7 @@
         return carry
 
     lax.fori_loop(0, BOXES, mine, 0)
-    for copy in nodes:
-        copy.wait()
-    tables = (a_ref, b_ref, row_ref, col_ref)
-    prepare(sources, rows, cols, tables)
-    make_weights(1, 1, targets, tables, high, low)
+    make_weights(1, 1, targets, (a_ref, b_ref, row_ref, col_ref), high, low)
 
 
 def between_kernel(
@@ -444,16 +446,18 @@
             name="pack",
         )(far(current), *nodes)
         got = swapped(packed, "sy")
-        partial, row0, col0, a_near, b_near = pl.pallas_call(
+        sources1, targets1, rows1, cols1 = node_buffers(None)
+        partial, row0, col0, a_near, b_near, *tables1 = pl.pallas_call(
             near_kernel,
-            in_specs=[WHOLE] * 3,
-            out_specs=[WHOLE] * 5,
-            out_shape=[KEPT, SPREAD, SPREAD, COLUMNS, COLUMNS],
-            scratch_shapes=(PAIR, PAIR),
+            in_specs=[WHOLE] * 3 + [ANY] * 4,
+            out_specs=[WHOLE] * 10,
+            out_shape=[KEPT, SPREAD, SPREAD, COLUMNS, COLUMNS]
+            + [COLUMNS, COLUMNS, SPREAD, SPREAD, targets1],
+            scratch_shapes=(PAIR, PAIR, sources1, rows1, cols1, pltpu.SemaphoreType.DMA((4,))),
             compiler_params=PARAMS,
             cost_estimate=cost(20_000_000),
             name="near",
-        )(packed, rows, cols)
+        )(packed, rows, cols, *nodes)
         sent, a_got, b_got = pl.pallas_call(
             partner_kernel,
             in_specs=[WHOLE] * 4,
@@ -465,16 +469,14 @@
         )(got, row0, col0, partial)
         own, high, low = pl.pallas_call(
             second_kernel,
-            in_specs=[WHOLE] * 8 + [ANY] * 4,
+            in_specs=[WHOLE] * 13,
             out_specs=[WHOLE] * 3,
             out_shape=[KEPT, MADE, MADE],
-            scratch_shapes=node_buffers(None)
-            + TABLES
-            + (PAIR, PAIR, pltpu.SemaphoreType.DMA((4,))),
+            scratch_shapes=(PAIR, PAIR),
             compiler_params=PARAMS,
             cost_estimate=cost(60_000_000),
             name="second",
-        )(packed, got, row0, col0, a_near, b_near, a_got, b_got, *nodes)
+        )(packed, got, row0, col0, a_near, b_near, a_got, b_got, *tables1)
         pieces = swapped(sent, "sx")
         sent, current = pl.pallas_call(
             middle_kernel,

time: 40.4 us -> 41.2 us (1.020)
  the two profiles are of different devices: /device:TPU:16 before, /device:TPU:2 now
where the time goes in v7:
time: 41.2 us; the launch traced here: 40.8 us
  starting transfers between devices  15.2 us (37%)
  Pallas kernels  13.4 us (33%)
  blocking collectives  11 us (27%)
  waiting for transfers between devices  1.11 us (3%)
    all_to_all x1, blocking collectives, exchange(): lax.all_to_all(sent, ('sx', 'sy'), 0, 0, axis_index_groups=groups[level],...  11 us
    all_to_all x1, starting transfers between devices, exchange(): lax.all_to_all(sent, ('sx', 'sy'), 0, 0, axis_index_groups=groups[level],...  9.25 us
    ppermute x2, starting transfers between devices, swapped(): return lax.ppermute(block, axis, [(i, i ^ 1) for i in range(count)])  5.96 us
    pallas_call x1, Pallas kernels, local(): pl.pallas_call(between_kernel, in_specs=[WHOLE] + [ANY] * 4, out_specs=[W...  4.41 us
    pallas_call x1, Pallas kernels, local(): pl.pallas_call(second_kernel, in_specs=[WHOLE] * 13, out_specs=[WHOLE] *...  3.02 us
    pallas_call x1, Pallas kernels, local(): pl.pallas_call(near_kernel, in_specs=[WHOLE] * 3 + [ANY] * 4, out_specs=[...  1.67 us
    pallas_call x1, Pallas kernels, local(): pl.pallas_call(middle_kernel, in_specs=[WHOLE] * 4, out_specs=[ANY, WHOLE...  1.3 us
    pallas_call x1, Pallas kernels, local(): pl.pallas_call(pack_kernel, in_specs=[ANY] * 5, out_specs=[WHOLE] * 3, ou...  0.9 us
  transfers between devices with their start and end apart: 3, of which 2 were waited for; matrix products, arithmetic and copies ran while one was open for 0% of the time, Pallas kernels for 22%

profile of v7, /device:TPU:2, one launch (start us, length us, event | category | flops | bytes accessed | tf_op | source)
XLA Modules:
  0.0 40.8 jit_solution(10015654660522148477)
XLA Ops:
  0.0 0.9 %pack.1 = (f32[88,256]{1,0:T(8,128)S(1)}, f32[2,16,16]{2,1,0:T(8,128)S(1)}, f32[2,16,16]{2,1,0:T(8,128)S(1)}) custom-call(f32[2,2,16,256]{3,2,1,0:T(8,128)} %bitcast.4, f32[3,2,2,1,256]{4,3,2,1,0:T(1,128)} %sources_hbm.5, f32[3,2,2,2,2,1,256]{6,5,4,3,2,1,0:T(1,128)} %targets_hbm.5, f32[3,2,16,16]{3,2,1,0:T(8,128)} %rows_hbm.5, f32[3,2,16,16]{3,2,1,0:T(8,128)} %cols_hbm.5), custom_call_target="tpu_custom_call" | custom-call | tf_op jit(solution)/shard_map/pack/pallas_call | solution.py:439
  0.9 1.9 %collective-permute-start = (f32[88,256]{1,0:T(8,128)S(1)}, f32[88,256]{1,0:T(8,128)S(1)}, u32[]{:S(2)}, u32[]{:S(2)}) collective-permute-start(f32[88,256]{1,0:T(8,128)S(1)} %get-tuple-element.31.packed), channel_id=1, source_target_pairs={{0,1},{1,0},{2,3},{3,2},{4,5},{5,4},{6,7},{7,6},{8,9},{9,8},{10,11... | collective-permute-start | bytes 270344 | tf_op jit(solution)/shard_map/ppermute | solution.py:51
  2.8 1.7 %near.1 = (f32[2,2,16,256]{3,2,1,0:T(8,128)S(1)}, f32[2,16,256]{2,1,0:T(8,128)S(1)}, f32[2,16,256]{2,1,0:T(8,128)S(1)}, f32[2,256,128]{2,1,0:T(8,128)S(1)}, f32[...) custom-call(f32[88,256]{1,0:T(8,128)S(1)} %get-tuple-element.31.pack, ...), custom_call_target="tpu_custom_call" | custom-call | flops 20000000 | bytes 100000 | tf_op jit(solution)/shard_map/near/pallas_call | solution.py:450
  4.5 0.0 collective-permute-done.packed.got
  4.5 0.8 %partner.1 = (f32[2,2,16,256]{3,2,1,0:T(8,128)S(1)}, f32[2,256,128]{2,1,0:T(8,128)S(1)}, f32[2,256,128]{2,1,0:T(8,128)S(1)}) custom-call(f32[88,256]{1,0:T(8,128)S(1)} %collective-permute-done.packed.got, f32[2,16,256]{2,1,0:T(8,128)S(1)} %get-tuple-element.34.row_ref.row0_ref, f32[2,16,256]{2,1,0:T(8,128)S(1)} %get-tuple-element.35.col_ref.col0_ref, ...), custom_call_target="tpu_custom_call" | custom-call | tf_op jit(solution)/shard_map/partner/pallas_call | solution.py:461
  5.4 4.0 %collective-permute-start.1 = (f32[2,2,16,256]{3,2,1,0:T(8,128)S(1)}, f32[2,2,16,256]{3,2,1,0:T(8,128)S(1)}, u32[]{:S(2)}, u32[]{:S(2)}) collective-permute-start(f32[2,2,16,256]{3,2,1,0:T(8,128)S(1)} %get-tuple-element.37), channel_id=1, source_target_pairs={{0,32},{32,0},{64,96},{96,64},{128,160},{160,128},{192,224},{224,1... | collective-permute-start | bytes 196616 | tf_op jit(solution)/shard_map/ppermute | solution.py:51
  9.4 3.0 %second.1 = (f32[2,2,16,256]{3,2,1,0:T(8,128)S(1)}, bf16[6,512,256]{2,1,0:T(8,128)(2,1)S(1)}, bf16[6,512,256]{2,1,0:T(8,128)(2,1)S(1)}) custom-call(f32[88,256]{1,0:T(8,128)S(1)} %get-tuple-element.31.packed, f32[88,256]{1,0:T(8,128)S(1)} %collective-permute-done.packed.got, f32[2,16,256]{2,1,0:T(8,128)S(1)} %get-tuple-element.34.row_ref.row0_ref, ...), custom_call_target="tpu_custom_call" | custom-call | flops 60000000 | bytes 100000 | tf_op jit(solution)/shard_map/second/pallas_call | solution.py:470
  12.5 0.8 %collective-permute-done.1.piece = f32[2,2,16,256]{3,2,1,0:T(8,128)S(1)} collective-permute-done((f32[2,2,16,256]{3,2,1,0:T(8,128)S(1)}, f32[2,2,16,256]{3,2,1,0:T(8,128)S(1)}, u32[]{:S(2)}, u32[]{:S(2)}) %collective-permute-start.1) | collective-permute-done | bytes 65568 | tf_op jit(solution)/shard_map/ppermute | solution.py:51
  13.3 1.3 %middle.1 = (f32[4,2,2,16,256]{4,3,2,1,0:T(8,128)}, f32[2,2,16,256]{3,2,1,0:T(8,128)S(1)}) custom-call(f32[2,2,16,256]{3,2,1,0:T(8,128)S(1)} %collective-permute-done.1.piece, f32[2,2,16,256]{3,2,1,0:T(8,128)S(1)} %get-tuple-element.47.own, bf16[6,512,256]{2,1,0:T(8,128)(2,1)S(1)} %get-tuple-element.48.high, bf16[6,512,256]{2,1,0:T(8,128)(2,1)S(1)} %get-tuple-element.49.low), custom_call_target="tpu_custom_call" | custom-call | tf_op jit(solution)/shard_map/middle/pallas_call | solution.py:481
  14.6 9.3 %all-to-all-start = ((f32[4,2,2,16,256]{4,3,2,1,0:T(8,128)}), f32[4,2,2,16,256]{4,3,2,1,0:T(8,128)S(1)}, u32[]{:S(2)}, u32[]{:S(2)}) async-start(f32[4,2,2,16,256]{4,3,2,1,0:T(8,128)} %get-tuple-element.50), calls=%async_computation | async-start | bytes 524288 | tf_op jit(solution)/shard_map/all_to_all | solution.py:427
  23.9 4.4 %between.1 = (f32[2,2,16,256]{3,2,1,0:T(8,128)S(1)}, bf16[8,512,256]{2,1,0:T(8,128)(2,1)S(1)}, f8e4m3fn[8,512,256]{2,1,0:T(32,128)(4,1)S(1)}, f32[2,128]{1,0:T(2,128)S(1)}, f32[2,128]{1,0:T(2,128)S(1)}) custom-call(f32[2,2,16,256]{3,2,1,0:T(8,128)S(1)} %get-tuple-element.51.values, f32[3,2,2,1,256]{4,3,2,1,0:T(1,128)} %sources_hbm.5, ...), custom_call_target="tpu_custom_call" | custom-call | flops 60000000 | bytes 100000 | tf_op jit(solution)/shard_map/between/pallas_call | solution.py:490
  28.3 0.3 all-to-all-done.pieces
  28.6 0.6 %late.1 = f32[4,2,2,16,256]{4,3,2,1,0:T(8,128)S(1)} custom-call(f32[4,2,2,16,256]{4,3,2,1,0:T(8,128)S(1)} %all-to-all-done.pieces, f32[2,2,16,256]{3,2,1,0:T(8,128)S(1)} %get-tuple-element.52.own, bf16[8,512,256]{2,1,0:T(8,128)(2,1)S(1)} %get-tuple-element.53.high, f8e4m3fn[8,512,256]{2,1,0:T(32,128)(4,1)S(1)} %get-tuple-element.54.low, ...), custom_call_target="tpu_custom_call" | custom-call | tf_op jit(solution)/shard_map/late/pallas_call | solution.py:509
  29.1 11.0 %all_to_all.10.pieces = f32[4,2,2,16,256]{4,3,2,1,0:T(8,128)S(1)} all-to-all(f32[4,2,2,16,256]{4,3,2,1,0:T(8,128)S(1)} %late.1), channel_id=1, replica_groups={{0,4,128,132},{1,5,129,133},{2,6,130,134},{3,7,131,135},{8,12,136,140},..., dimensions={0} | all-to-all | bytes 524288 | tf_op jit(solution)/shard_map/all_to_all | solution.py:427
  40.1 0.6 %final.1 = f32[2,2,16,256]{3,2,1,0:T(8,128)} custom-call(f32[4,2,2,16,256]{4,3,2,1,0:T(8,128)S(1)} %all_to_all.10.pieces), custom_call_target="tpu_custom_call" | custom-call | tf_op jit(solution)/shard_map/final/pallas_call | solution.py:518
Async XLA Ops:
  0.9 3.6 %collective-permute-start = (f32[88,256]{1,0:T(8,128)S(1)}, f32[88,256]{1,0:T(8,128)S(1)}, u32[]{:S(2)}, u32[]{:S(2)}) collective-permute-start(f32[88,256]{1,0:T(8,128)S(1)} %get-tuple-element.31.packed), channel_id=1, source_target_pairs={{0,1},{1,0},{2,3},{3,2},{4,5},{5,4},{6,7},{7,6},{8,9},{9,8},{10,11... | collective-permute-start | bytes 270344 | tf_op jit(solution)/shard_map/ppermute | solution.py:51
  5.4 7.9 %collective-permute-start.1 = (f32[2,2,16,256]{3,2,1,0:T(8,128)S(1)}, f32[2,2,16,256]{3,2,1,0:T(8,128)S(1)}, u32[]{:S(2)}, u32[]{:S(2)}) collective-permute-start(f32[2,2,16,256]{3,2,1,0:T(8,128)S(1)} %get-tuple-element.37), channel_id=1, source_target_pairs={{0,32},{32,0},{64,96},{96,64},{128,160},{160,128},{192,224},{224,1... | collective-permute-start | bytes 196616 | tf_op jit(solution)/shard_map/ppermute | solution.py:51
  14.6 14.0 %all-to-all-start = ((f32[4,2,2,16,256]{4,3,2,1,0:T(8,128)}), f32[4,2,2,16,256]{4,3,2,1,0:T(8,128)S(1)}, u32[]{:S(2)}, u32[]{:S(2)}) async-start(f32[4,2,2,16,256]{4,3,2,1,0:T(8,128)} %get-tuple-element.50), calls=%async_computation | async-start | bytes 524288 | tf_op jit(solution)/shard_map/all_to_all | solution.py:427
